TPU v7x, 128 devices: a whole 4x4x4 slice. The times are simulated.
128 devices in a mesh: leaf: 128 (over z, y, x, core).
Axes of the slice: x: 4, y: 4, z: 4, core: 2. Of those that a mesh axis runs over, the one named last changes fastest.
Arguments:
- points: float32 [524288, 128], P('leaf')
- right_side: float32 [64, 524288], P(None, 'leaf'), may hold values from -6 to 6
- neighbours: int32 [1024, 5], P('leaf'), may hold values from -1 to 1023, as said below
- leaf_interp: float32 [1024, 512, 256], P('leaf'), may hold values from -0.25 to 0.25
- leaf_skeleton: int32 [1024, 256], P('leaf'), may hold values from 0 to 511, as said below
- node_skeleton: int32 [1022, 256], replicated, may hold values from 0 to 511, as said below
- node_gain: float32 [2046, 256], replicated, may hold values from 0.5 to 1.5
- transfer: float32 [9, 2, 256, 256], replicated, may hold values from -0.1875 to 0.1875
Outputs:
- solution: float32 [64, 524288], P(None, 'leaf')
- residual: float32 [64, 524288], P(None, 'leaf')
Inputs may be any that keep to these rules, and one draw needn't show every extreme that they name: `neighbours`: slot s of leaf j holds j + s - 2 or -1, and slot 2 holds j; leaf m stands in leaf j's list exactly when j stands in leaf m's. `leaf_skeleton`: the entries of a row are distinct. `node_skeleton`: the entries of a row are distinct.
All inputs are finite; a program needn't handle non-finite values.
Results may differ from a plain program's by a relative error of at most 0.0003.
Values sent between devices are 32-bit elements; how exact they have to be, the bound alone decides.
A program may use at most 192 MiB of HBM per device.

v0:
```python
import functools

import jax
import jax.numpy as jnp
from jax import lax
from jax.sharding import Mesh
from jax.sharding import PartitionSpec as P

ITERS = 2
LEAF = ("leaf_0", "leaf_1", "leaf_2", "leaf_3")


highest = lax.Precision.HIGHEST
ridge = 1.0


def padded(cells, sides, width):
    for axis, dim in sides:
        count = lax.axis_size(axis)
        ends = count - 1
        head = lax.slice_in_dim(cells, 0, width, axis=dim)
        tail = lax.slice_in_dim(cells, cells.shape[dim] - width, cells.shape[dim], axis=dim)
        cells = jnp.concatenate(
            [
                lax.ppermute(tail, axis, [(i, (i + 1) % count) for i in range(ends)]),
                cells,
                lax.ppermute(head, axis, [((i + 1) % count, i) for i in range(ends)]),
            ],
            axis=dim,
        )
    return cells


def swapped(block, axis, stride):
    count = lax.axis_size(axis)
    route = []
    for low in range(count):
        high = low | 1 << stride
        if high != low and high < count:
            route += [(low, high), (high, low)]
    return lax.ppermute(block, axis, route)


def over_axes(x, axes):
    return functools.reduce(lax.psum, axes, x)


def pair_kernel(first_set, second_set):
    inner = jnp.einsum("nqd,npd->nqp", first_set, second_set, precision=highest)
    first_norm = jnp.sum(first_set * first_set, axis=-1)
    second_norm = jnp.sum(second_set * second_set, axis=-1)
    return jnp.exp((2.0 * inner - first_norm[:, :, None] - second_norm[:, None, :]) * 0.5)


def symmetric(matrix):
    return 0.5 * (matrix + matrix.T)


def chol_apply(matrix, target):
    factor = jnp.linalg.cholesky(matrix)
    return jax.scipy.linalg.cho_solve((factor, True), target)


def body(
    points, right_side, neighbours, leaf_interp, leaf_skeleton, node_skeleton, node_gain, transfer
):
    leaf_count, slot_count = neighbours.shape
    reach = (slot_count - 1) // 2
    leaf_size = leaf_interp.shape[1]
    skel_size = leaf_interp.shape[2]
    coord_dim = points.shape[1]
    classes = right_side.shape[0]
    dev_count = lax.axis_size(LEAF)
    dev_levels = dev_count.bit_length() - 1
    local_levels = leaf_count.bit_length() - 1
    levels = local_levels + dev_levels
    leaves = leaf_count * dev_count
    device_index = lax.axis_index(LEAF)
    rows_here = leaf_count * leaf_size

    def gain_first(level):
        return 2 * leaves - 2 * (leaves >> level)

    def skel_first(level):
        return leaves - 2 * (leaves >> level)

    own_points = points.reshape(leaf_count, leaf_size, coord_dim)
    extended_points = padded(points, ((LEAF, 0),), reach * leaf_size)
    near_mask = (neighbours >= 0).astype(jnp.float32)
    near_tiles = []
    for slot_id in range(slot_count):
        neighbour = extended_points[slot_id * leaf_size : slot_id * leaf_size + rows_here].reshape(
            leaf_count, leaf_size, coord_dim
        )
        near_tiles.append(pair_kernel(neighbour, own_points) * near_mask[:, slot_id, None, None])
    skel_points = jnp.take_along_axis(own_points, leaf_skeleton[:, :, None], axis=1)
    local_far = []
    for level in range(local_levels):
        node_count = leaf_count >> level
        paired = skel_points.reshape(node_count // 2, 2, skel_size, coord_dim)
        sibling = paired[:, ::-1].reshape(node_count, skel_size, coord_dim)
        local_far.append(pair_kernel(sibling, skel_points))
        picked = lax.dynamic_slice_in_dim(
            node_skeleton,
            skel_first(level + 1) + device_index * (node_count // 2),
            node_count // 2,
            0,
        )
        skel_points = jnp.take_along_axis(
            paired.reshape(node_count // 2, 2 * skel_size, coord_dim), picked[:, :, None], axis=1
        )
    own_skel = skel_points[0]
    device_far = []
    for level_bit in range(dev_levels):
        level = local_levels + level_bit
        partner = swapped(own_skel, LEAF, level_bit)
        device_far.append(pair_kernel(partner[None], own_skel[None])[0])
        if level + 1 < levels:
            is_right = device_index >> level_bit & 1
            left_part = jnp.where(is_right == 0, own_skel, partner)
            right_part = jnp.where(is_right == 0, partner, own_skel)
            picked = lax.dynamic_slice_in_dim(
                node_skeleton, skel_first(level + 1) + (device_index >> level_bit + 1), 1, 0
            )[0]
            own_skel = jnp.take(jnp.concatenate([left_part, right_part], axis=0), picked, axis=0)
    solution = jnp.zeros_like(right_side)
    residual = right_side
    direction = right_side
    res_norm = symmetric(over_axes(jnp.dot(residual, residual.T, precision=highest), LEAF))
    for step in range(ITERS):
        extended = padded(direction, ((LEAF, 1),), reach * leaf_size)
        near = jnp.zeros((classes, leaf_count, leaf_size), jnp.float32)
        for operate_slot_id in range(slot_count):
            shifted = extended[
                :, operate_slot_id * leaf_size : operate_slot_id * leaf_size + rows_here
            ].reshape(classes, leaf_count, leaf_size)
            near = near + jnp.einsum(
                "cnq,nqp->cnp", shifted, near_tiles[operate_slot_id], precision=highest
            )
        by_leaf = direction.reshape(classes, leaf_count, leaf_size)
        weights = jnp.einsum("cnq,nqs->ncs", by_leaf, leaf_interp, precision=highest)
        local_sibling = []
        for operate_level in range(local_levels):
            operate_node_count = leaf_count >> operate_level
            operate_paired = weights.reshape(operate_node_count // 2, 2, classes, skel_size)
            local_sibling.append(
                operate_paired[:, ::-1].reshape(operate_node_count, classes, skel_size)
            )
            node_scale = lax.dynamic_slice_in_dim(
                node_gain,
                gain_first(operate_level) + device_index * operate_node_count,
                operate_node_count,
                0,
            )
            scaled = operate_paired * node_scale.reshape(operate_node_count // 2, 2, 1, skel_size)
            weights = jnp.einsum(
                "ncs,st->nct", scaled[:, 0], transfer[operate_level, 0], precision=highest
            )
            weights = weights + jnp.einsum(
                "ncs,st->nct", scaled[:, 1], transfer[operate_level, 1], precision=highest
            )
        own_node = weights[0]
        device_sibling = []
        for operate_level_bit in range(dev_levels):
            operate_level = local_levels + operate_level_bit
            operate_partner = swapped(own_node, LEAF, operate_level_bit)
            device_sibling.append(operate_partner)
            if operate_level + 1 < levels:
                operate_is_right = device_index >> operate_level_bit & 1
                node_scale = lax.dynamic_slice_in_dim(
                    node_gain,
                    gain_first(operate_level) + 2 * (device_index >> operate_level_bit + 1),
                    2,
                    0,
                )
                operate_left_part = (
                    jnp.where(operate_is_right == 0, own_node, operate_partner) * node_scale[0]
                )
                operate_right_part = (
                    jnp.where(operate_is_right == 0, operate_partner, own_node) * node_scale[1]
                )
                own_node = jnp.dot(operate_left_part, transfer[operate_level, 0], precision=highest)
                own_node = own_node + jnp.dot(
                    operate_right_part, transfer[operate_level, 1], precision=highest
                )
        potential = jnp.dot(device_sibling[-1], device_far[-1], precision=highest)
        for operate_level_bit in range(dev_levels - 2, -1, -1):
            operate_level = local_levels + operate_level_bit
            operate_is_right = device_index >> operate_level_bit & 1
            down_map = jnp.where(
                operate_is_right == 0, transfer[operate_level, 0], transfer[operate_level, 1]
            )
            node_scale = lax.dynamic_index_in_dim(
                node_gain,
                gain_first(operate_level) + (device_index >> operate_level_bit),
                0,
                keepdims=False,
            )
            potential = jnp.dot(potential, down_map.T, precision=highest) * node_scale
            potential = potential + jnp.dot(
                device_sibling[operate_level_bit], device_far[operate_level_bit], precision=highest
            )
        potential = potential[None]
        for operate_level in range(local_levels - 1, -1, -1):
            operate_node_count = leaf_count >> operate_level
            children = jnp.stack(
                [
                    jnp.einsum(
                        "nct,st->ncs", potential, transfer[operate_level, 0], precision=highest
                    ),
                    jnp.einsum(
                        "nct,st->ncs", potential, transfer[operate_level, 1], precision=highest
                    ),
                ],
                axis=1,
            )
            node_scale = lax.dynamic_slice_in_dim(
                node_gain,
                gain_first(operate_level) + device_index * operate_node_count,
                operate_node_count,
                0,
            )
            children = (
                children.reshape(operate_node_count, classes, skel_size) * node_scale[:, None, :]
            )
            potential = children + jnp.einsum(
                "ncs,nst->nct",
                local_sibling[operate_level],
                local_far[operate_level],
                precision=highest,
            )
        far = jnp.einsum("ncs,nqs->cnq", potential, leaf_interp, precision=highest)
        image = (
            ridge * direction + near.reshape(classes, rows_here) + far.reshape(classes, rows_here)
        )
        curvature = symmetric(over_axes(jnp.dot(direction, image.T, precision=highest), LEAF))
        alpha_mat = chol_apply(curvature, res_norm)
        solution = solution + jnp.dot(alpha_mat.T, direction, precision=highest)
        residual = residual - jnp.dot(alpha_mat.T, image, precision=highest)
        if step + 1 < ITERS:
            new_norm = symmetric(over_axes(jnp.dot(residual, residual.T, precision=highest), LEAF))
            beta_mat = chol_apply(res_norm, new_norm)
            direction = residual + jnp.dot(beta_mat.T, direction, precision=highest)
            res_norm = new_norm
    return (solution, residual)


def solution(mesh):
    torus = Mesh(mesh.devices.reshape(4, 4, 4, 2), ("leaf_0", "leaf_1", "leaf_2", "leaf_3"))
    in_specs = (
        P(LEAF, None),
        P(None, LEAF),
        P(LEAF, None),
        P(LEAF, None, None),
        P(LEAF, None),
        P(),
        P(),
        P(),
    )
    out_specs = (P(None, LEAF), P(None, LEAF))
    return jax.shard_map(body, mesh=torus, in_specs=in_specs, out_specs=out_specs, check_vma=False)
```

profile of v0, /device:TPU:0, one launch (start us, length us, event | category | flops | bytes accessed | tf_op | source)
XLA Modules:
  0.0 689.4 jit_solution(11426544796465122347)
XLA Ops:
  29.4 22.7 %gather_fusion.1 = f32[2048,128]{1,0:T(8,128)} fusion(f32[8,512,128]{2,1,0:T(8,128)S(1)} %bitcast.557, s32[2048]{0:T(1024)S(1)} %bitcast.563), kind=kCustom, calls=%fused_computation.7 | custom fusion | bytes 2113536 | tf_op jit(solution)/shard_map/jit(take_along_axis)/gather | solution.py:96
  54.6 16.1 %gather_fusion.2 = f32[1024,128]{1,0:T(8,128)} fusion(f32[4,512,128]{2,1,0:T(8,128)} %broadcast_select_fusion.1, s32[1024]{0:T(1024)S(1)} %bitcast.566), kind=kCustom, calls=%fused_computation.8 | custom fusion | bytes 1056768 | tf_op jit(solution)/shard_map/jit(take_along_axis)/gather | solution.py:109
  72.8 8.4 %gather_fusion.3 = f32[512,128]{1,0:T(8,128)} fusion(f32[2,512,128]{2,1,0:T(8,128)} %broadcast_select_fusion.3, s32[512]{0:T(512)S(1)} %bitcast.573), kind=kCustom, calls=%fused_computation.9 | custom fusion | bytes 528384 | tf_op jit(solution)/shard_map/jit(take_along_axis)/gather | solution.py:109
  116.0 9.2 %fusion.414 = f32[8,512,512]{2,1,0:T(8,128)} fusion(f32[8,512,128]{2,1,0:T(8,128)S(1)} %bitcast.558), kind=kOutput, calls=%fused_computation.695 | convolution fusion | flops 3221225472 | bytes 10485760 | tf_op jit(solution)/shard_map/nqd,npd->nqp/dot_general | solution.py:49
  245.9 10.2 %fusion.413 = f32[8,512,512]{2,1,0:T(8,128)} fusion(f32[8,512,128]{2,1,0:T(8,128)} %bitcast.599, f32[8,512,128]{2,1,0:T(8,128)S(1)} %bitcast.559), kind=kOutput, calls=%fused_computation.694 | convolution fusion | flops 3221225472 | bytes 12582912 | tf_op jit(solution)/shard_map/nqd,npd->nqp/dot_general | solution.py:49
  256.2 9.0 %fusion.412 = f32[8,512,512]{2,1,0:T(8,128)} fusion(f32[8,512,128]{2,1,0:T(8,128)S(1)} %bitcast.598, f32[8,512,128]{2,1,0:T(8,128)S(1)} %bitcast.560), kind=kOutput, calls=%fused_computation.693 | convolution fusion | flops 3221225472 | bytes 12582912 | tf_op jit(solution)/shard_map/nqd,npd->nqp/dot_general | solution.py:49
  265.2 6.7 fusion.416
  272.0 8.9 %fusion.415 = f32[8,512,512]{2,1,0:T(8,128)} fusion(f32[8,512,128]{2,1,0:T(8,128)S(1)} %bitcast.596, f32[8,512,128]{2,1,0:T(8,128)S(1)} %bitcast.562), kind=kOutput, calls=%fused_computation.696 | convolution fusion | flops 3221225472 | bytes 12582912 | tf_op jit(solution)/shard_map/nqd,npd->nqp/dot_general | solution.py:49
  281.0 10.4 %fusion.1 = f32[8,512,64]{1,2,0:T(8,128)S(1)} fusion(f32[8,512,512]{2,1,0:T(8,128)} %fusion.412, f32[8]{0:T(128)S(1)} %copy-done.143, f32[8,512]{1,0:T(8,128)S(1)} %sub.269, f32[8,512]{1,0:T(8,128)S(1)} %sub.266, f32[8,8,8,512]{3,2,1,0:T(8,128)S(1)} %bitcast.618), kind=kOutput, calls=%fused_computation.16 | convolution fusion | flops 1621098496 | bytes 10518560 | tf_op jit(solution)/shard_map/cnq,nqp->cnp/dot_general | solution.py:137
  291.4 10.0 %fusion.72 = f32[8,512,64]{1,2,0:T(8,128)S(1)} fusion(f32[8,512,64]{1,2,0:T(8,128)S(1)} %fusion.1, f32[8,512,512]{2,1,0:T(8,128)} %fusion.413, f32[8]{0:T(128)S(1)} %copy-done.141, f32[8,512]{1,0:T(8,128)S(1)} %sub.272, f32[8,512]{1,0:T(8,128)S(1)} %sub.269, f32[8,8,8,512]{3,2,1,0:T(8,128)S(1)} %bitcast.617), kind=kOutput, calls=%fused_computation.100 | convolution fusion | flops 1621360640 | bytes 11567136 | tf_op jit(solution)/shard_map/cnq,nqp->cnp/dot_general | solution.py:137
  301.4 8.0 %fusion.70 = f32[8,512,64]{1,2,0:T(8,128)S(1)} fusion(f32[8,512,64]{1,2,0:T(8,128)S(1)} %fusion.72, f32[8,512,512]{2,1,0:T(8,128)S(1)} %bitcast.591, f32[8]{0:T(128)S(1)} %copy-done.139, f32[8,512]{1,0:T(8,128)S(1)} %sub.269, f32[8,8,8,512]{3,2,1,0:T(8,128)S(1)} %bitcast.565), kind=kOutput, calls=%fused_computation.98 | convolution fusion | flops 1621360640 | bytes 11550752 | tf_op jit(solution)/shard_map/cnq,nqp->cnp/dot_general | solution.py:137
  309.5 10.1 %fusion.68 = f32[8,512,64]{1,2,0:T(8,128)S(1)} fusion(f32[8,512,64]{1,2,0:T(8,128)S(1)} %fusion.70, f32[8,512,512]{2,1,0:T(8,128)} %fusion.415, f32[8]{0:T(128)S(1)} %copy-done.137, f32[8,512]{1,0:T(8,128)S(1)} %sub.279, f32[8,512]{1,0:T(8,128)S(1)} %sub.269, f32[8,8,8,512]{3,2,1,0:T(8,128)S(1)} %bitcast.616), kind=kOutput, calls=%fused_computation.96 | convolution fusion | flops 1621360640 | bytes 11567136 | tf_op jit(solution)/shard_map/cnq,nqp->cnp/dot_general | solution.py:137
  319.7 8.8 %fusion.65 = f32[8,8,8,512]{3,2,1,0:T(8,128)S(1)} fusion(f32[8,512,64]{1,2,0:T(8,128)S(1)} %fusion.68, f32[8,512,512]{2,1,0:T(8,128)S(1)} %fusion.416, f32[8]{0:T(128)S(1)} %copy-done.135, f32[8,512]{1,0:T(8,128)S(1)} %copy-done.88, f32[8,512]{1,0:T(8,128)} %copy-done.86, f32[8,8,8,512]{3,2,1,0:T(8,128)S(1)} %bitcast.615), kind=kOutput, calls=%fused_computation.93 | convolution fusion | flops 1621360640 | bytes 11567136 | tf_op jit(solution)/shard_map/cnq,nqp->cnp/dot_general | solution.py:137
  342.7 5.4 collective-permute-done.17
  381.5 14.9 %all-reduce.2 = (f32[64,64]{1,0:T(8,128)S(1)}, f32[64,64]{1,0:T(8,128)S(1)}) all-reduce(f32[64,64]{1,0:T(8,128)S(1)} %copy-done.72, f32[64,64]{1,0:T(8,128)S(1)} %convolution_bitcast_fusion.14), channel_id=1, replica_groups=mesh['leaf_0'=4,'leaf_1'=4,'leaf_2'=4,'leaf_3'=2] {'leaf_0'}, use_global_device_ids=true, to_apply=%region_31.34 | all-reduce | flops 8192 | bytes 65536 | tf_op jit(solution)/shard_map/psum | solution.py:45
  396.4 15.4 %all-reduce.1 = (f32[64,64]{1,0:T(8,128)S(1)}, f32[64,64]{1,0:T(8,128)S(1)}) all-reduce(f32[64,64]{1,0:T(8,128)S(1)} %get-tuple-element.20, f32[64,64]{1,0:T(8,128)S(1)} %get-tuple-element.21), channel_id=1, replica_groups=mesh['leaf_0'=4,'leaf_1'=4,'leaf_2'=4,'leaf_3'=2] {'leaf_1'}, use_global_device_ids=true, to_apply=%region_32.35 | all-reduce | flops 8192 | bytes 65536 | tf_op jit(solution)/shard_map/psum | solution.py:45
  411.8 18.0 %all-reduce = (f32[64,64]{1,0:T(8,128)S(1)}, f32[64,64]{1,0:T(8,128)}) all-reduce(f32[64,64]{1,0:T(8,128)S(1)} %get-tuple-element.18, f32[64,64]{1,0:T(8,128)S(1)} %get-tuple-element.19), channel_id=1, replica_groups=mesh['leaf_0'=4,'leaf_1'=4,'leaf_2'=4,'leaf_3'=2] {'leaf_2'}, use_global_device_ids=true, to_apply=%region_33.36 | all-reduce | flops 8192 | bytes 65536 | tf_op jit(solution)/shard_map/psum | solution.py:45
  434.2 5.8 cholesky.70
  441.3 5.5 custom-call.16
  447.7 6.6 cholesky.59
  464.2 15.1 %psum.120 = f32[64,64]{1,0:T(8,128)S(1)} all-reduce(f32[64,64]{1,0:T(8,128)S(1)} %fusion.420), channel_id=1, replica_groups=mesh['leaf_0'=4,'leaf_1'=4,'leaf_2'=4,'leaf_3'=2] {'leaf_0'}, use_global_device_ids=true, to_apply=%region_35.39 | all-reduce | flops 4096 | bytes 32768 | tf_op jit(solution)/shard_map/psum | solution.py:45
  479.4 14.9 %psum.121 = f32[64,64]{1,0:T(8,128)S(1)} all-reduce(f32[64,64]{1,0:T(8,128)S(1)} %psum.120), channel_id=1, replica_groups=mesh['leaf_0'=4,'leaf_1'=4,'leaf_2'=4,'leaf_3'=2] {'leaf_1'}, use_global_device_ids=true, to_apply=%region_36.40 | all-reduce | flops 4096 | bytes 32768 | tf_op jit(solution)/shard_map/psum | solution.py:45
  494.3 15.8 %psum.122 = f32[64,64]{1,0:T(8,128)S(1)} all-reduce(f32[64,64]{1,0:T(8,128)S(1)} %psum.121), channel_id=1, replica_groups=mesh['leaf_0'=4,'leaf_1'=4,'leaf_2'=4,'leaf_3'=2] {'leaf_2'}, use_global_device_ids=true, to_apply=%region_37.41 | all-reduce | flops 4096 | bytes 32768 | tf_op jit(solution)/shard_map/psum | solution.py:45
  547.1 11.0 %fusion = f32[8,512,64]{1,2,0:T(8,128)S(1)} fusion(f32[8,512,512]{2,1,0:T(8,128)} %fusion.412, f32[8]{0:T(128)} %get-tuple-element.15, f32[8,512]{1,0:T(8,128)} %copy-done.86, f32[8,512]{1,0:T(8,128)} %copy-done.94, f32[8,8,8,512]{3,2,1,0:T(8,128)S(1)} %bitcast.622), kind=kOutput, calls=%fused_computation.15 | convolution fusion | flops 1621098496 | bytes 10518560 | tf_op jit(solution)/shard_map/cnq,nqp->cnp/dot_general | solution.py:137
  558.2 9.9 %fusion.73 = f32[8,512,64]{1,2,0:T(8,128)S(1)} fusion(f32[8,512,64]{1,2,0:T(8,128)S(1)} %fusion, f32[8,512,512]{2,1,0:T(8,128)} %fusion.413, f32[8]{0:T(128)S(1)} %copy-done.142, f32[8,512]{1,0:T(8,128)S(1)} %copy-done.93, f32[8,512]{1,0:T(8,128)S(1)} %copy-done.87, f32[8,8,8,512]{3,2,1,0:T(8,128)S(1)} %bitcast.621), kind=kOutput, calls=%fused_computation.101 | convolution fusion | flops 1621360640 | bytes 11567136 | tf_op jit(solution)/shard_map/cnq,nqp->cnp/dot_general | solution.py:137
  573.3 8.0 %fusion.71 = f32[8,512,64]{1,2,0:T(8,128)S(1)} fusion(f32[8,512,64]{1,2,0:T(8,128)S(1)} %fusion.73, f32[8,512,512]{2,1,0:T(8,128)S(1)} %bitcast.593, f32[8]{0:T(128)S(1)} %copy-done.140, f32[8,512]{1,0:T(8,128)S(1)} %copy-done.87, f32[8,8,8,512]{3,2,1,0:T(8,128)S(1)} %bitcast.568), kind=kOutput, calls=%fused_computation.99 | convolution fusion | flops 1621360640 | bytes 11550752 | tf_op jit(solution)/shard_map/cnq,nqp->cnp/dot_general | solution.py:137
  584.6 9.9 %fusion.69 = f32[8,512,64]{1,2,0:T(8,128)S(1)} fusion(f32[8,512,64]{1,2,0:T(8,128)S(1)} %fusion.71, f32[8,512,512]{2,1,0:T(8,128)} %fusion.415, f32[8]{0:T(128)S(1)} %copy-done.138, f32[8,512]{1,0:T(8,128)S(1)} %copy-done.91, f32[8,512]{1,0:T(8,128)S(1)} %copy-done.87, f32[8,8,8,512]{3,2,1,0:T(8,128)S(1)} %bitcast.620), kind=kOutput, calls=%fused_computation.97 | convolution fusion | flops 1621360640 | bytes 11567136 | tf_op jit(solution)/shard_map/cnq,nqp->cnp/dot_general | solution.py:137
  596.7 8.0 %fusion.67 = f32[8,8,8,512]{3,2,1,0:T(8,128)S(1)} fusion(f32[8,512,64]{1,2,0:T(8,128)S(1)} %fusion.69, f32[8,512,512]{2,1,0:T(8,128)S(1)} %bitcast.595, f32[8]{0:T(128)S(1)} %copy-done.136, f32[8,512]{1,0:T(8,128)S(1)} %copy-done.89, f32[8,512]{1,0:T(8,128)S(1)} %copy-done.87, f32[8,8,8,512]{3,2,1,0:T(8,128)S(1)} %bitcast.619), kind=kOutput, calls=%fused_computation.95 | convolution fusion | flops 1621360640 | bytes 11567136 | tf_op jit(solution)/shard_map/cnq,nqp->cnp/dot_general | solution.py:137
  619.9 15.6 %psum.124 = f32[64,64]{1,0:T(8,128)S(1)} all-reduce(f32[64,64]{1,0:T(8,128)S(1)} %fusion.138), channel_id=1, replica_groups=mesh['leaf_0'=4,'leaf_1'=4,'leaf_2'=4,'leaf_3'=2] {'leaf_0'}, use_global_device_ids=true, to_apply=%region_39.43 | all-reduce | flops 4096 | bytes 32768 | tf_op jit(solution)/shard_map/psum | solution.py:45
  635.5 17.3 %psum.125 = f32[64,64]{1,0:T(8,128)S(1)} all-reduce(f32[64,64]{1,0:T(8,128)S(1)} %psum.124), channel_id=1, replica_groups=mesh['leaf_0'=4,'leaf_1'=4,'leaf_2'=4,'leaf_3'=2] {'leaf_1'}, use_global_device_ids=true, to_apply=%region_40.44 | all-reduce | flops 4096 | bytes 32768 | tf_op jit(solution)/shard_map/psum | solution.py:45
  652.8 14.7 %psum.126 = f32[64,64]{1,0:T(8,128)S(1)} all-reduce(f32[64,64]{1,0:T(8,128)S(1)} %psum.125), channel_id=1, replica_groups=mesh['leaf_0'=4,'leaf_1'=4,'leaf_2'=4,'leaf_3'=2] {'leaf_2'}, use_global_device_ids=true, to_apply=%region_41.45 | all-reduce | flops 4096 | bytes 32768 | tf_op jit(solution)/shard_map/psum | solution.py:45
  671.1 5.8 cholesky.81
  (636 shorter events, 328.9 us)
Async XLA Ops:
  18.6 132.6 %collective-permute-start.4 = (f32[64,256]{1,0:T(8,128)}, f32[64,256]{1,0:T(8,128)}, u32[]{:S(2)}, u32[]{:S(2)}) collective-permute-start(f32[64,256]{1,0:T(8,128)} %convolution_add_fusion.37), channel_id=1, source_target_pairs={{0,1},{1,0},{2,3},{3,2},{4,5},{5,4},{6,7},{7,6},{8,9},{9,8},{10,11... | collective-permute-start | bytes 196616 | tf_op jit(solution)/shard_map/ppermute | solution.py:41
  19.5 177.4 %collective-permute-start.3 = (f32[64,1024]{1,0:T(8,128)}, f32[64,1024]{1,0:T(8,128)}, u32[]{:S(2)}, u32[]{:S(2)}) collective-permute-start(f32[64,1024]{1,0:T(8,128)} %get-tuple-element.77), channel_id=1, source_target_pairs={{1,0},{2,1},{3,2},{4,3},{5,4},{6,5},{7,6},{8,7},{9,8},{10,9},{11,1... | collective-permute-start | bytes 786440 | tf_op jit(solution)/shard_map/ppermute | solution.py:27
  20.8 173.1 %collective-permute-start.1 = (f32[64,1024]{1,0:T(8,128)}, f32[64,1024]{1,0:T(8,128)}, u32[]{:S(2)}, u32[]{:S(2)}) collective-permute-start(f32[64,1024]{1,0:T(8,128)} %get-tuple-element.78), channel_id=1, source_target_pairs={{0,1},{1,2},{2,3},{3,4},{4,5},{5,6},{6,7},{7,8},{8,9},{9,10},{10,1... | collective-permute-start | bytes 786440 | tf_op jit(solution)/shard_map/ppermute | solution.py:25
  84.6 80.1 %collective-permute-start.11 = (f32[256,128]{1,0:T(8,128)}, f32[256,128]{1,0:T(8,128)}, u32[]{:S(2)}, u32[]{:S(2)}) collective-permute-start(f32[256,128]{1,0:T(8,128)} %broadcast_select_fusion.11), channel_id=1, source_target_pairs={{0,1},{1,0},{2,3},{3,2},{4,5},{5,4},{6,7},{7,6},{8,9},{9,8},{10,11... | collective-permute-start | bytes 393224 | tf_op jit(solution)/shard_map/ppermute | solution.py:41
  86.6 147.1 %collective-permute-start.2 = (f32[1024,128]{1,0:T(8,128)}, f32[1024,128]{1,0:T(8,128)}, u32[]{:S(2)}, u32[]{:S(2)}) collective-permute-start(f32[1024,128]{1,0:T(8,128)} %get-tuple-element.42), channel_id=1, source_target_pairs={{1,0},{2,1},{3,2},{4,3},{5,4},{6,5},{7,6},{8,7},{9,8},{10,9},{11,1... | collective-permute-start | bytes 1572872 | tf_op jit(solution)/shard_map/ppermute | solution.py:27
  153.7 5.2 collective-permute-start.5
  158.9 70.5 %collective-permute-start = (f32[1024,128]{1,0:T(8,128)}, f32[1024,128]{1,0:T(8,128)}, u32[]{:S(2)}, u32[]{:S(2)}) collective-permute-start(f32[1024,128]{1,0:T(8,128)} %get-tuple-element.43), channel_id=1, source_target_pairs={{0,1},{1,2},{2,3},{3,4},{4,5},{5,6},{6,7},{7,8},{8,9},{9,10},{10,1... | collective-permute-start | bytes 1572872 | tf_op jit(solution)/shard_map/ppermute | solution.py:25
  164.7 8.6 %collective-permute-start.6 = (f32[64,256]{1,0:T(8,128)}, f32[64,256]{1,0:T(8,128)}, u32[]{:S(2)}, u32[]{:S(2)}) collective-permute-start(f32[64,256]{1,0:T(8,128)} %convolution_add_fusion.35), channel_id=1, source_target_pairs={{0,4},{4,0},{1,5},{5,1},{2,6},{6,2},{3,7},{7,3},{8,12},{12,8},{9,1... | collective-permute-start | bytes 196616 | tf_op jit(solution)/shard_map/ppermute | solution.py:41
  175.8 6.2 collective-permute-start.7
  182.0 5.4 collective-permute-start.12
  187.4 14.7 %collective-permute-start.8 = (f32[64,256]{1,0:T(8,128)}, f32[64,256]{1,0:T(8,128)}, u32[]{:S(2)}, u32[]{:S(2)}) collective-permute-start(f32[64,256]{1,0:T(8,128)} %convolution_add_fusion.33), channel_id=1, source_target_pairs={{0,16},{16,0},{1,17},{17,1},{2,18},{18,2},{3,19},{19,3},{4,20},{20... | collective-permute-start | bytes 196616 | tf_op jit(solution)/shard_map/ppermute | solution.py:41
  193.9 13.9 %collective-permute-start.13 = (f32[256,128]{1,0:T(8,128)S(1)}, f32[256,128]{1,0:T(8,128)S(1)}, u32[]{:S(2)}, u32[]{:S(2)}) collective-permute-start(f32[256,128]{1,0:T(8,128)S(1)} %get-tuple-element.27), channel_id=1, source_target_pairs={{0,4},{4,0},{1,5},{5,1},{2,6},{6,2},{3,7},{7,3},{8,12},{12,8},{9,1... | collective-permute-start | bytes 393224 | tf_op jit(solution)/shard_map/ppermute | solution.py:41
  205.3 9.1 %collective-permute-start.9 = (f32[64,256]{1,0:T(8,128)}, f32[64,256]{1,0:T(8,128)}, u32[]{:S(2)}, u32[]{:S(2)}) collective-permute-start(f32[64,256]{1,0:T(8,128)} %convolution_add_fusion.32), channel_id=1, source_target_pairs={{0,32},{32,0},{1,33},{33,1},{2,34},{34,2},{3,35},{35,3},{4,36},{36... | collective-permute-start | bytes 196616 | tf_op jit(solution)/shard_map/ppermute | solution.py:41
  211.7 9.5 %collective-permute-start.14 = (f32[256,128]{1,0:T(8,128)S(1)}, f32[256,128]{1,0:T(8,128)S(1)}, u32[]{:S(2)}, u32[]{:S(2)}) collective-permute-start(f32[256,128]{1,0:T(8,128)S(1)} %get-tuple-element.29), channel_id=1, source_target_pairs={{0,8},{8,0},{1,9},{9,1},{2,10},{10,2},{3,11},{11,3},{4,12},{12,4},... | collective-permute-start | bytes 393224 | tf_op jit(solution)/shard_map/ppermute | solution.py:41
  217.5 131.1 %collective-permute-start.10 = (f32[64,256]{1,0:T(8,128)}, f32[64,256]{1,0:T(8,128)}, u32[]{:S(2)}, u32[]{:S(2)}) collective-permute-start(f32[64,256]{1,0:T(8,128)} %convolution_add_fusion.31), channel_id=1, source_target_pairs={{0,64},{64,0},{1,65},{65,1},{2,66},{66,2},{3,67},{67,3},{4,68},{68... | collective-permute-start | bytes 196616 | tf_op jit(solution)/shard_map/ppermute | solution.py:41
  225.1 104.9 %copy-start.41 = (f32[256,128]{1,0:T(8,128)}, f32[256,128]{1,0:T(8,128)S(1)}, u32[]{:S(2)}) copy-start(f32[256,128]{1,0:T(8,128)S(1)} %get-tuple-element.31) | copy-start | bytes 393220
  225.1 104.9 %collective-permute-start.15 = (f32[256,128]{1,0:T(8,128)S(1)}, f32[256,128]{1,0:T(8,128)}, u32[]{:S(2)}, u32[]{:S(2)}) collective-permute-start(f32[256,128]{1,0:T(8,128)S(1)} %get-tuple-element.31), channel_id=1, source_target_pairs={{0,16},{16,0},{1,17},{17,1},{2,18},{18,2},{3,19},{19,3},{4,20},{20... | collective-permute-start | bytes 393224 | tf_op jit(solution)/shard_map/ppermute | solution.py:41
  233.7 75.7 %copy-start.86 = (f32[8,512]{1,0:T(8,128)}, f32[8,512]{1,0:T(8,128)S(1)}, u32[]{:S(2)}) copy-start(f32[8,512]{1,0:T(8,128)S(1)} %sub.269) | copy-start | bytes 49156
  241.0 68.4 %copy-start.90 = (f32[8,512]{1,0:T(8,128)}, f32[8,512]{1,0:T(8,128)S(1)}, u32[]{:S(2)}) copy-start(f32[8,512]{1,0:T(8,128)S(1)} %sub.279) | copy-start | bytes 49156
  333.0 5.0 collective-permute-start.16
  341.3 6.8 collective-permute-start.17
  380.2 80.6 %copy-start.11 = (f32[8,8,8,512]{3,2,0,1:T(8,128)}, f32[8,8,8,512]{3,2,0,1:T(8,128)S(1)}, u32[]{:S(2)}) copy-start(f32[8,8,8,512]{3,2,0,1:T(8,128)S(1)} %copy.77) | copy-start | bytes 3145732
  447.0 67.1 %copy-start.73 = (f32[1,64,64]{1,2,0:T(8,128)S(1)}, f32[1,64,64]{1,2,0:T(8,128)}, u32[]{:S(2)}) copy-start(f32[1,64,64]{1,2,0:T(8,128)} %custom-call.16) | copy-start | bytes 49156
  524.9 1.3 collective-permute-start.20
  527.1 4.4 collective-permute-start.21
  532.1 10.1 %collective-permute-start.22 = (f32[64,256]{1,0:T(8,128)S(1)}, f32[64,256]{1,0:T(8,128)S(1)}, u32[]{:S(2)}, u32[]{:S(2)}) collective-permute-start(f32[64,256]{1,0:T(8,128)S(1)} %convolution_add_fusion.22), channel_id=1, source_target_pairs={{0,4},{4,0},{1,5},{5,1},{2,6},{6,2},{3,7},{7,3},{8,12},{12,8},{9,1... | collective-permute-start | bytes 196616 | tf_op jit(solution)/shard_map/ppermute | solution.py:41
  537.9 8.6 %collective-permute-start.19 = (f32[64,1024]{1,0:T(8,128)S(1)}, f32[64,1024]{1,0:T(8,128)S(1)}, u32[]{:S(2)}, u32[]{:S(2)}) collective-permute-start(f32[64,1024]{1,0:T(8,128)S(1)} %get-tuple-element.75), channel_id=1, source_target_pairs={{1,0},{2,1},{3,2},{4,3},{5,4},{6,5},{7,6},{8,7},{9,8},{10,9},{11,1... | collective-permute-start | bytes 786440 | tf_op jit(solution)/shard_map/ppermute | solution.py:27
  539.2 7.4 %collective-permute-start.18 = (f32[64,1024]{1,0:T(8,128)S(1)}, f32[64,1024]{1,0:T(8,128)S(1)}, u32[]{:S(2)}, u32[]{:S(2)}) collective-permute-start(f32[64,1024]{1,0:T(8,128)S(1)} %get-tuple-element.76), channel_id=1, source_target_pairs={{0,1},{1,2},{2,3},{3,4},{4,5},{5,6},{6,7},{7,8},{8,9},{9,10},{10,1... | collective-permute-start | bytes 786440 | tf_op jit(solution)/shard_map/ppermute | solution.py:25
  544.7 23.4 %collective-permute-start.23 = (f32[64,256]{1,0:T(8,128)S(1)}, f32[64,256]{1,0:T(8,128)S(1)}, u32[]{:S(2)}, u32[]{:S(2)}) collective-permute-start(f32[64,256]{1,0:T(8,128)S(1)} %convolution_add_fusion.21), channel_id=1, source_target_pairs={{0,8},{8,0},{1,9},{9,1},{2,10},{10,2},{3,11},{11,3},{4,12},{12,4},... | collective-permute-start | bytes 196616 | tf_op jit(solution)/shard_map/ppermute | solution.py:41
  568.7 12.6 %collective-permute-start.24 = (f32[64,256]{1,0:T(8,128)S(1)}, f32[64,256]{1,0:T(8,128)S(1)}, u32[]{:S(2)}, u32[]{:S(2)}) collective-permute-start(f32[64,256]{1,0:T(8,128)S(1)} %convolution_add_fusion.20), channel_id=1, source_target_pairs={{0,16},{16,0},{1,17},{17,1},{2,18},{18,2},{3,19},{19,3},{4,20},{20... | collective-permute-start | bytes 196616 | tf_op jit(solution)/shard_map/ppermute | solution.py:41
  581.9 12.7 %collective-permute-start.25 = (f32[64,256]{1,0:T(8,128)S(1)}, f32[64,256]{1,0:T(8,128)S(1)}, u32[]{:S(2)}, u32[]{:S(2)}) collective-permute-start(f32[64,256]{1,0:T(8,128)S(1)} %convolution_add_fusion.19), channel_id=1, source_target_pairs={{0,32},{32,0},{1,33},{33,1},{2,34},{34,2},{3,35},{35,3},{4,36},{36... | collective-permute-start | bytes 196616 | tf_op jit(solution)/shard_map/ppermute | solution.py:41
  595.1 9.8 %collective-permute-start.26 = (f32[64,256]{1,0:T(8,128)S(1)}, f32[64,256]{1,0:T(8,128)S(1)}, u32[]{:S(2)}, u32[]{:S(2)}) collective-permute-start(f32[64,256]{1,0:T(8,128)S(1)} %convolution_add_fusion.18), channel_id=1, source_target_pairs={{0,64},{64,0},{1,65},{65,1},{2,66},{66,2},{3,67},{67,3},{4,68},{68... | collective-permute-start | bytes 196616 | tf_op jit(solution)/shard_map/ppermute | solution.py:41
  (149 other events, 1807.9 us)
where the time goes:
time: 702 us; the launch traced here: 689 us
  matrix products  261 us (37%)
  blocking collectives  153 us (22%)
  other arithmetic  101 us (14%)
  local copies, waits for them, and re-layouts  99.6 us (14%)
  starting transfers between devices  52.6 us (7%)
  waiting for transfers between devices  18 us (3%)
    psum x12, blocking collectives, over_axes(): return functools.reduce(lax.psum, axes, x)  153 us
    dot_general x10, matrix products, body(): jnp.einsum('cnq,nqp->cnp', shifted, near_tiles[operate_slot_id], precisio...  94.2 us
    dot_general x15, matrix products, pair_kernel(): inner = jnp.einsum('nqd,npd->nqp', first_set, second_set, precision=highest)  62.8 us
    ppermute x21, starting transfers between devices, swapped(): return lax.ppermute(block, axis, route)  39.2 us
    gather x3, local copies, waits for them, and re-layouts, body(): jnp.take_along_axis(paired.reshape(node_count // 2, 2 * skel_size, coord_...  25.4 us
    gather x1, local copies, waits for them, and re-layouts, body(): jnp.take_along_axis(own_points, leaf_skeleton[:, :, None], axis=1)  22.7 us
    another operation x9, other arithmetic, chol_apply(): factor = jnp.linalg.cholesky(matrix)  20.3 us
    ppermute x21, waiting for transfers between devices, swapped(): return lax.ppermute(block, axis, route)  18 us
  transfers between devices with their start and end apart: 27, of which 7 were waited for; matrix products, arithmetic and copies ran while one was open for 48% of the time, Pallas kernels for 0%

commit v1 on v0

v1 whole, which is shorter than its diff:
```python
import functools

import jax
import jax.numpy as jnp
from jax import lax
from jax.experimental import pallas as pl
from jax.experimental.pallas import tpu as pltpu
from jax.sharding import PartitionSpec as P

MESH = pl.DeviceIdType.MESH
F32 = jnp.float32
BF16 = jnp.bfloat16
I32 = jnp.int32

LEAF, SKEL, DIM, CLS = 512, 256, 128, 64
LV = 8
LEAVES = 1024
HALF = CLS // 2
OWN = 2 * LEAF
WIDE = (LV + 4) * LEAF


def split(x):
    high = x.astype(BF16)
    return high, (x - high.astype(F32)).astype(BF16)


def dot(a, b, ca=1, cb=0):
    return lax.dot_general(a, b, (((ca,), (cb,)), ((), ())), preferred_element_type=F32)


def times(stacked, high, low, cb=0):
    rows = stacked.shape[0] // 2
    both = dot(stacked, high, 1, cb)
    return both[:rows] + both[rows:] + dot(stacked[:rows], low, 1, cb)


def stack(x):
    return jnp.concatenate(split(x), axis=0)


def times_f32(a, b, cb=0):
    high, low = split(b)
    return times(stack(a), high, low, cb)


def norm_columns(x):
    half = -0.5 * jnp.sum(x * x, axis=1, keepdims=True)
    half = jnp.broadcast_to(half, x.shape)
    first = half.astype(BF16).astype(F32)
    rest = half - first
    second = rest.astype(BF16).astype(F32)
    third = rest - second
    lane = lax.broadcasted_iota(I32, x.shape, 1)
    parts = jnp.where(lane % 3 == 0, first, jnp.where(lane % 3 == 1, second, third))
    ones = jnp.ones_like(parts)
    zero = jnp.zeros_like(parts)
    low = jnp.where(lane < 3, ones, jnp.where(lane < 6, parts, zero))
    high = jnp.where(lane < 3, parts, jnp.where(lane < 6, ones, zero))
    return low.astype(BF16), high.astype(BF16)


def exponent(a_hl, a_n1, b_hl, b_n2):
    a_h = a_hl[:, :DIM]
    b_h, b_l = b_hl[:, :DIM], b_hl[:, DIM:]
    first = dot(a_hl, jnp.concatenate([b_h, b_h], axis=1), 1, 1)
    second = dot(
        jnp.concatenate([a_h, a_n1], axis=1), jnp.concatenate([b_l, b_n2], axis=1), 1, 1
    )
    return first + second


def transposed(top):
    return jnp.concatenate([top, jnp.zeros_like(top)], axis=0).T


def solve(matrix, target):
    work = jnp.concatenate([matrix, target], axis=1)
    row_id = lax.broadcasted_iota(I32, work.shape, 0)
    block = 4
    for start in range(0, CLS, block):
        columns = [
            jnp.broadcast_to(work[:, start + i : start + i + 1], work.shape) for i in range(block)
        ]
        for i in range(block):
            k = start + i
            here = row_id == k
            inverse = 1.0 / columns[i][k : k + 1, :]
            pivot = work[k : k + 1, :] * inverse
            work = jnp.where(here, pivot, work - columns[i] * pivot)
            for j in range(i + 1, block):
                entry = columns[j][k : k + 1, :] * inverse
                columns[j] = jnp.where(here, entry, columns[j] - columns[i] * entry)
    return work


def body(
    points, right_side, neighbours, leaf_interp, leaf_skeleton, node_skeleton, node_gain, transfer,
    x_out, r_out,
    xe, xhl, n1, n2, tile_h, tile_l, be, ye, near, dirn, vs, itp, tra, gw, nw, lsk, idx_rows, idx_cols,
    fh, fl, s_r0, s_q, w_r0, w_q, u4, ar_r0, ar_q,
    local_sem, send_sem, recv_sem,
):
    me = lax.axis_index("leaf")
    core = me % 2
    chip = me // 2
    left = (me + 127) % 128
    right = (me + 1) % 128
    partner = me + 1 - 2 * core

    def peer(axis, s):
        stride = (2, 8, 32)[axis]
        at = (me // stride) % 4
        if s == 1:
            other = at + 1 - 2 * (at % 2)
        elif s == 2:
            other = at + 2 - 4 * (at // 2)
        else:
            other = 3 - at
        return me + (other - at) * stride

    def xor(n, s):
        if s == 1:
            return n + 1 - 2 * (n % 2)
        if s == 2:
            return n + 2 - 4 * ((n // 2) % 2)
        return xor(xor(n, 1), 2)

    loads = []

    def load(src, dst):
        copy = pltpu.make_async_copy(src, dst, local_sem.at[len(loads)])
        copy.start()
        loads.append(copy)
        return copy

    own_rows = pl.ds(OWN, LV * LEAF)
    load_points = load(points, xe.at[own_rows, :])
    load_b = load(right_side, be.at[:, own_rows])
    load_small = [load(leaf_skeleton, lsk)]

    def gain_row(level):
        return 2 * LEAVES - 2 * (LEAVES >> level)

    def skel_row(level):
        return LEAVES - 2 * (LEAVES >> level)

    gain_node = [me * 8, me * 4, me * 2, me, me // 2, me // 4, me // 8, me // 16, me // 32]
    for level in range(9):
        if level < 8:
            at = pl.multiple_of(gain_row(level) + (gain_node[level] // 8) * 8, 8)
            load_small.append(load(node_gain.at[pl.ds(at, 8), :], gw.at[level]))
        else:
            load_small.append(load(node_gain.at[pl.ds(2040, 6), :], gw.at[level, pl.ds(0, 6), :]))
    skel_node = [None, me * 4, me * 2, me, me // 2, me // 4, me // 8, me // 16]
    for level in range(1, 9):
        if level < 8:
            at = pl.multiple_of(skel_row(level) + (skel_node[level] // 8) * 8, 8)
            load_small.append(load(node_skeleton.at[pl.ds(at, 8), :], nw.at[level]))
        else:
            load_small.append(load(node_skeleton.at[pl.ds(1016, 6), :], nw.at[level, pl.ds(0, 6), :]))
    load_itp = load(leaf_interp, itp)
    load_tra = load(transfer, tra)

    peers = [partner, left, right] + [peer(a, s) for a in range(3) for s in (1, 2, 3)]
    barrier = pltpu.get_barrier_semaphore()
    for other in peers:
        pl.semaphore_signal(barrier, inc=1, device_id=(other,), device_id_type=MESH)
    pl.semaphore_wait(barrier, len(peers))

    sent = []

    def send(src, dst, device):
        k = len(sent)
        copy = pltpu.make_async_remote_copy(
            src_ref=src, dst_ref=dst, send_sem=send_sem.at[k], recv_sem=recv_sem.at[k],
            device_id=(device,), device_id_type=MESH,
        )
        copy.start()
        sent.append(copy)
        return copy

    def send_quad(buf, index, axis):
        return [send(buf.at[index, 0], buf.at[index, s], peer(axis, s)) for s in (1, 2, 3)]

    def arrive(copies):
        for copy in copies:
            copy.wait_recv()

    load_points.wait()
    first, last = pl.ds(OWN, OWN), pl.ds(OWN + (LV - 2) * LEAF, OWN)
    head, tail = pl.ds(0, OWN), pl.ds(OWN + LV * LEAF, OWN)
    halo_x = [send(xe.at[first, :], xe.at[tail, :], left), send(xe.at[last, :], xe.at[head, :], right)]
    load_b.wait()
    halo_b = [send(be.at[:, first], be.at[:, tail], left), send(be.at[:, last], be.at[:, head], right)]

    def prepare(e):
        rows = pl.ds(pl.multiple_of(e * LEAF, LEAF), LEAF)
        x = xe[rows, :]
        high, low = split(x)
        xhl[rows, :] = jnp.concatenate([high, low], axis=1)
        a, b = norm_columns(x)
        n1[rows, :] = a
        n2[rows, :] = b

    def split_columns(src, e):
        cols = pl.ds(pl.multiple_of(e * LEAF, LEAF), LEAF)
        high, low = split(src[:, cols])
        vs[pl.ds(0, CLS), cols] = high
        vs[pl.ds(CLS, CLS), cols] = low

    def loop(start, stop, f):
        def step(i, carry):
            f(i)
            return carry

        lax.fori_loop(start, stop, step, 0)

    def own_setup(e):
        prepare(e)
        split_columns(be, e)

    loop(2, 10, own_setup)

    for copy in load_small:
        copy.wait()
    idx_rows[...] = jnp.zeros_like(idx_rows)
    idx_rows[pl.ds(0, 8), :] = lsk[...].astype(F32)

    def put_index(slot, level, row, parity):
        index = nw[level, pl.ds(row, 1), :] + 256 * parity
        index = jnp.where(index >= 512, index - 512, index)
        idx_rows[pl.ds(slot, 1), :] = index.astype(F32)

    for i in range(4):
        put_index(8 + i, 1, (me * 4) % 8 + i, 0)
    for i in range(2):
        put_index(12 + i, 2, (me * 2) % 8 + i, 0)
    put_index(14, 3, me % 8, 0)
    put_index(15, 4, (me // 2) % 8, me % 2)
    n4, n6, n8 = me // 2, me // 8, me // 32
    quad_level = (4, 6, 8)
    quad_node = (n4, n6, n8)
    for q in range(3):
        level, node = quad_level[q], quad_node[q]
        parent = node // 2
        lv = min(level + 1, 8)
        base = 4 if level == 8 else 0
        put_index(16 + 3 * q, lv, base + parent % 8, node % 2)
        put_index(17 + 3 * q, lv, base + xor(parent, 1) % 8, node % 2)
        if q < 2:
            grand = parent // 2
            put_index(18 + 3 * q, level + 2, grand % 8, parent % 2)
    idx_cols[...] = idx_rows[...].T.astype(I32)

    def pick(slot, rows_hl):
        lane = lax.broadcasted_iota(I32, (SKEL, 2 * SKEL), 1)
        chosen = jnp.broadcast_to(idx_cols[:, slot : slot + 1], (SKEL, 2 * SKEL))
        one_hot = jnp.where(lane == chosen, 1.0, 0.0).astype(BF16)
        return dot(one_hot, rows_hl).astype(BF16)

    def joined(hl):
        return hl[:, :DIM].astype(F32) + hl[:, DIM:].astype(F32)

    def far_tile(slot, sibling_hl, own_hl):
        a1, _ = norm_columns(joined(sibling_hl))
        _, b2 = norm_columns(joined(own_hl))
        high, low = split(jnp.exp(exponent(sibling_hl, a1, own_hl, b2)))
        fh[slot] = high
        fl[slot] = low

    skel = [pick(j, xhl[pl.ds(OWN + j * LEAF, LEAF), :]) for j in range(LV)]
    slot, index = 0, 8
    while len(skel) > 1:
        parents = []
        for i in range(len(skel) // 2):
            far_tile(slot, skel[2 * i + 1], skel[2 * i])
            parents.append(pick(index, jnp.concatenate(skel[2 * i : 2 * i + 2], axis=0)))
            slot += 1
            index += 1
        skel = parents
    skel3 = skel[0]
    s_r0[0] = joined(skel3)
    copy_s = [send(s_r0.at[0], s_r0.at[1], partner)]

    def gain(level, node):
        row = node % 8
        return gw[level, pl.ds(row, 1), :]

    load_itp.wait()
    load_tra.wait()

    class Tree:
        pass

    def up_local(it):
        t = Tree()
        t.levels = []
        rows = []
        for j in range(LV):
            v = vs[:, pl.ds(OWN + j * LEAF, LEAF)]
            high, low = split(itp[j])
            rows.append(times(v, high, low))
        for level in range(3):
            t.levels.append(rows)
            count = len(rows)
            lefts = jnp.concatenate(
                [rows[n] * gain(level, me * count + n) for n in range(0, count, 2)], axis=0
            )
            rights = jnp.concatenate(
                [rows[n] * gain(level, me * count + n) for n in range(1, count, 2)], axis=0
            )
            joint = times_f32(lefts, tra[level, 0]) + times_f32(rights, tra[level, 1])
            rows = [joint[n * CLS : (n + 1) * CLS] for n in range(count // 2)]
        w_r0[it, 0] = rows[0]
        t.copies = [send(w_r0.at[it, 0], w_r0.at[it, 1], partner)]
        return t

    my_half = pl.ds(pl.multiple_of(core * HALF, HALF), HALF)

    def up_core(it, t):
        arrive(t.copies)
        own = w_r0[it, 0, my_half, :] * gain(3, me)
        sib = w_r0[it, 1, my_half, :] * gain(3, partner)
        w_q[it * 3, 0] = times_f32(own, tra[3, core]) + times_f32(sib, tra[3, 1 - core])
        t.copies = send_quad(w_q, it * 3, 0)
        t.sib = {}

    def up_quad(it, t, q):
        arrive(t.copies)
        level, node = quad_level[q], quad_node[q]
        parity = node % 2
        four = [w_q[it * 3 + q, s] for s in range(4)]
        t.sib[level] = four[1]
        if q == 2:
            a = four[2] * gain(level, xor(node, 2))
            b = four[3] * gain(level, xor(node, 3))
            t.sib[level + 1] = times_f32(a, tra[level, parity]) + times_f32(b, tra[level, 1 - parity])
            return
        a = jnp.concatenate([four[0] * gain(level, node), four[2] * gain(level, xor(node, 2))], axis=0)
        b = jnp.concatenate(
            [four[1] * gain(level, xor(node, 1)), four[3] * gain(level, xor(node, 3))], axis=0
        )
        two = times_f32(a, tra[level, parity]) + times_f32(b, tra[level, 1 - parity])
        t.sib[level + 1] = two[HALF:]
        parent = node // 2
        parity = parent % 2
        a = two[:HALF] * gain(level + 1, parent)
        b = two[HALF:] * gain(level + 1, xor(parent, 1))
        w_q[it * 3 + q + 1, 0] = times_f32(a, tra[level + 1, parity]) + times_f32(
            b, tra[level + 1, 1 - parity]
        )
        t.copies = send_quad(w_q, it * 3 + q + 1, q + 1)

    def down_top(it, t):
        pot = times(stack(t.sib[9]), fh[13], fl[13])
        for level in range(8, 3, -1):
            node = me // (1 << (level - 3))
            pot = times_f32(pot, tra[level, node % 2], 1) * gain(level, node)
            pot = pot + times(stack(t.sib[level]), fh[level + 4], fl[level + 4])
        u4[it, my_half, :] = pot
        t.copies = [send(u4.at[it, my_half, :], u4.at[it, my_half, :], partner)]

    def down_local(it, t, store):
        arrive(t.copies)
        pot = times_f32(u4[it], tra[3, core], 1) * gain(3, me)
        pot = pot + times(stack(w_r0[it, 1]), fh[7], fl[7])
        slot = 7
        for level in (2, 1, 0):
            rows = t.levels[level]
            count = len(rows)
            slot -= count // 2
            stacked = stack(pot)
            out = []
            lefts = times(stacked, *split(tra[level, 0]), 1)
            rights = times(stacked, *split(tra[level, 1]), 1)
            for n in range(count):
                part = (lefts, rights)[n % 2][(n // 2) * CLS : (n // 2 + 1) * CLS]
                part = part * gain(level, me * count + n)
                other = stack(rows[n + 1 - 2 * (n % 2)])
                f = slot + n // 2
                out.append(part + times(other, fh[f], fl[f], n % 2))
            pot = jnp.concatenate(out, axis=0)
        for j in range(LV):
            high, low = split(itp[j])
            store(j, times(stack(pot[j * CLS : (j + 1) * CLS]), high, low, 1))

    def skel_core():
        arrive(copy_s)
        other = jnp.concatenate(split(s_r0[1]), axis=1)
        far_tile(7, other, skel3)
        own = pick(15, jnp.concatenate([skel3, other], axis=0))
        s_q[0, 0] = joined(own)
        return own, send_quad(s_q, 0, 0)

    def skel_quad(q, own, copies):
        arrive(copies)
        s1, s2, s3 = [jnp.concatenate(split(s_q[q, s]), axis=1) for s in (1, 2, 3)]
        far_tile(8 + 2 * q, s1, own)
        mine = pick(16 + 3 * q, jnp.concatenate([own, s1], axis=0))
        theirs = pick(17 + 3 * q, jnp.concatenate([s2, s3], axis=0))
        far_tile(9 + 2 * q, theirs, mine)
        if q == 2:
            return None, None
        up = pick(18 + 3 * q, jnp.concatenate([mine, theirs], axis=0))
        s_q[q + 1, 0] = joined(up)
        return up, send_quad(s_q, q + 1, q + 1)

    def build(t):
        e = (t + 6) // 3
        k = (t + 6) % 3
        rows = pl.ds(pl.multiple_of(e * LEAF, LEAF), LEAF)
        cols = pl.ds(pl.multiple_of((e + k) * LEAF, LEAF), LEAF)
        if isinstance(t, int):
            flag = neighbours[e - 2, 2 + k] if e >= 2 else neighbours[e + k - 2, 2 - k]
        else:
            flag = neighbours[e - 2, 2 + k]
        mask = jnp.where(flag >= 0, 1.0, 0.0).astype(F32)
        high, low = split(jnp.exp(exponent(xhl[rows, :], n1[rows, :], xhl[cols, :], n2[cols, :])) * mask)
        tile_h[t + 4] = high
        tile_l[t + 4] = low

    def near_target(out, j):
        total = None
        for o in (0, -1, -2, 1, 2):
            cols = pl.ds(pl.multiple_of((j + 2 + o) * LEAF, LEAF), LEAF)
            t = 3 * j + o if o >= 0 else 3 * (j + o) - o
            part = times(vs[:, cols], tile_h[t + 4], tile_l[t + 4], 1 if o > 0 else 0)
            total = part if total is None else total + part
        return total

    def gram(pairs):
        sums = None
        for j in range(LV):
            stacks = {}

            def get(ref, at):
                if id(ref) not in stacks:
                    stacks[id(ref)] = stack(ref[:, pl.ds(at + j * LEAF, LEAF)])
                return stacks[id(ref)]

            parts = []
            for a, a0, b, b0 in pairs:
                bs = get(b, b0)
                parts.append(times(get(a, a0), bs[:CLS], bs[CLS:], 1))
            sums = parts if sums is None else [s + p for s, p in zip(sums, parts)]
        return sums

    class Sum:
        pass

    def sum_start(index, value):
        r = Sum()
        rows = value.shape[0]
        r.rows, r.index = pl.ds(0, rows), index
        ar_r0[index, 0, r.rows, :] = value
        r.copies = [send(ar_r0.at[index, 0, r.rows, :], ar_r0.at[index, 1, r.rows, :], partner)]
        return r

    def sum_step(r, stage):
        arrive(r.copies)
        if stage == 0:
            value = ar_r0[r.index, 0, r.rows, :] + ar_r0[r.index, 1, r.rows, :]
        else:
            at = r.index * 3 + stage - 1
            value = (ar_q[at, 0, r.rows, :] + ar_q[at, 1, r.rows, :]) + (
                ar_q[at, 2, r.rows, :] + ar_q[at, 3, r.rows, :]
            )
        if stage < 3:
            at = r.index * 3 + stage
            ar_q[at, 0, r.rows, :] = value
            r.copies = [
                send(ar_q.at[at, 0, r.rows, :], ar_q.at[at, s, r.rows, :], peer(stage, s)) for s in (1, 2, 3)
            ]
        return value

    def folded(m):
        return jnp.concatenate([m[:HALF], m[HALF:]], axis=1)

    def unfolded(m):
        return jnp.concatenate([m[:, :CLS], m[:, CLS:]], axis=0)

    t0 = up_local(0)
    sum0 = sum_start(0, folded(gram([(be, OWN, be, OWN)])[0]))
    loop(0, 5, build)
    up_core(0, t0)
    own4, copy_s = skel_core()
    sum_step(sum0, 0)
    loop(5, 10, build)
    up_quad(0, t0, 0)
    own6, copy_s = skel_quad(0, own4, copy_s)
    sum_step(sum0, 1)
    loop(10, 15, build)
    up_quad(0, t0, 1)
    own8, copy_s = skel_quad(1, own6, copy_s)
    sum_step(sum0, 2)
    loop(15, 20, build)
    up_quad(0, t0, 2)
    skel_quad(2, own8, copy_s)
    m0 = unfolded(sum_step(sum0, 3))
    down_top(0, t0)
    arrive(halo_x)

    def halo_setup(e):
        prepare(e)

    loop(0, 2, halo_setup)
    loop(10, 12, halo_setup)
    loop(20, 24, build)
    for t in (-4, -2, -1):
        build(t)

    def store_first(j, far):
        cols = pl.ds(OWN + j * LEAF, LEAF)
        ye[:, cols] = far + be[:, cols]

    down_local(0, t0, store_first)
    arrive(halo_b)

    def split_b(e):
        split_columns(be, e)

    loop(0, 2, split_b)
    loop(10, 12, split_b)

    def first_near(j):
        cols = pl.ds(pl.multiple_of((j + 2) * LEAF, LEAF), LEAF)
        ye[:, cols] = ye[:, cols] + near_target(ye, j)

    loop(0, LV, first_near)

    halo_y = [send(ye.at[:, first], ye.at[:, tail], left), send(ye.at[:, last], ye.at[:, head], right)]

    def split_y(e):
        split_columns(ye, e)

    loop(2, 10, split_y)
    t1 = up_local(1)
    sum1 = sum_start(1, jnp.concatenate(gram([(be, OWN, ye, OWN), (ye, OWN, ye, OWN)]), axis=1))

    def second_near(j):
        cols = pl.ds(pl.multiple_of(j * LEAF, LEAF), LEAF)
        near[:, cols] = near_target(near, j)

    loop(2, 4, second_near)
    up_core(1, t1)
    sum_step(sum1, 0)
    loop(4, 5, second_near)
    up_quad(1, t1, 0)
    sum_step(sum1, 1)
    loop(5, 6, second_near)
    up_quad(1, t1, 1)
    sum_step(sum1, 2)
    arrive(halo_y)
    loop(0, 2, split_y)
    loop(10, 12, split_y)
    loop(0, 2, second_near)
    up_quad(1, t1, 2)
    down_top(1, t1)
    moments = sum_step(sum1, 3)
    loop(6, 8, second_near)

    def store_second(j, far):
        cols = pl.ds(j * LEAF, LEAF)
        near[:, cols] = near[:, cols] + far + ye[:, pl.ds(OWN + j * LEAF, LEAF)]

    down_local(1, t1, store_second)

    def square_t(m):
        return jnp.concatenate([m, jnp.zeros_like(m)], axis=1)

    def sym(m):
        return 0.5 * (m + transposed(square_t(m))[:CLS, :CLS])

    m0 = sym(m0)
    m1 = moments[:, :CLS]
    m2 = moments[:, CLS:]
    step = solve(sym(m1), m0)
    alpha = step[:, CLS:]
    alpha_t = transposed(step)[CLS:, :CLS]
    cross = times_f32(m1, alpha)
    new = m0 - 2.0 * sym(cross) + sym(times_f32(times_f32(alpha_t, m2), alpha))
    beta_t = transposed(solve(m0, new))[CLS:, :CLS]
    row = lax.broadcasted_iota(I32, (CLS, CLS), 0)
    col = lax.broadcasted_iota(I32, (CLS, CLS), 1)
    plus_t = jnp.where(row == col, 1.0, 0.0) + beta_t

    alpha_s = stack(alpha_t)
    plus_s = stack(plus_t)

    def mix(matrix_s, x):
        high, low = split(x)
        return times(matrix_s, high, low)

    def make_second(j):
        cols = pl.ds(pl.multiple_of(j * LEAF, LEAF), LEAF)
        wide = pl.ds(pl.multiple_of((j + 2) * LEAF, LEAF), LEAF)
        dirn[:, cols] = mix(plus_s, be[:, wide]) - mix(alpha_s, ye[:, wide])
        near[:, cols] = mix(plus_s, ye[:, wide]) - mix(alpha_s, near[:, cols])

    loop(0, LV, make_second)
    curve = sum_start(2, folded(gram([(dirn, 0, near, 0)])[0]))

    def first_update(j):
        wide = pl.ds(pl.multiple_of((j + 2) * LEAF, LEAF), LEAF)
        old = be[:, wide]
        be[:, wide] = mix(alpha_s, old)
        ye[:, wide] = old - mix(alpha_s, ye[:, wide])

    sum_step(curve, 0)
    for copy in halo_b + halo_y:
        copy.wait_send()
    loop(0, LV, first_update)
    sum_step(curve, 1)
    sum_step(curve, 2)
    curvature = sym(unfolded(sum_step(curve, 3)))
    last_t = transposed(solve(curvature, new))[CLS:, :CLS]
    last_s = stack(last_t)

    def last_update(j):
        cols = pl.ds(pl.multiple_of(j * LEAF, LEAF), LEAF)
        wide = pl.ds(pl.multiple_of((j + 2) * LEAF, LEAF), LEAF)
        be[:, wide] = be[:, wide] + mix(last_s, dirn[:, cols])
        ye[:, wide] = ye[:, wide] - mix(last_s, near[:, cols])

    loop(0, LV, last_update)
    outs = [load(be.at[:, own_rows], x_out), load(ye.at[:, own_rows], r_out)]
    for copy in outs:
        copy.wait()
    for copy in sent:
        if not any(copy is done for done in halo_b + halo_y):
            copy.wait_send()


def solution(mesh):
    any_space = pl.BlockSpec(memory_space=pl.ANY)
    vmem = pltpu.VMEM

    def device(points, right_side, neighbours, leaf_interp, leaf_skeleton, node_skeleton, node_gain, transfer):
        out = jax.ShapeDtypeStruct(right_side.shape, F32)
        return pl.pallas_call(
            body,
            out_shape=(out, out),
            in_specs=[
                any_space, any_space, pl.BlockSpec(memory_space=pltpu.SMEM), any_space,
                any_space, any_space, any_space, any_space,
            ],
            out_specs=(any_space, any_space),
            scratch_shapes=[
                vmem((WIDE, DIM), F32),
                vmem((WIDE, 2 * DIM), BF16),
                vmem((WIDE, DIM), BF16),
                vmem((WIDE, DIM), BF16),
                vmem((28, LEAF, LEAF), BF16),
                vmem((28, LEAF, LEAF), BF16),
                vmem((CLS, WIDE), F32),
                vmem((CLS, WIDE), F32),
                vmem((CLS, LV * LEAF), F32),
                vmem((CLS, LV * LEAF), F32),
                vmem((2 * CLS, WIDE), BF16),
                vmem((LV, LEAF, SKEL), F32),
                vmem((9, 2, SKEL, SKEL), F32),
                vmem((9, 8, SKEL), F32),
                vmem((9, 8, SKEL), I32),
                vmem((LV, SKEL), I32),
                vmem((128, SKEL), F32),
                vmem((SKEL, 128), I32),
                vmem((14, SKEL, SKEL), BF16),
                vmem((14, SKEL, SKEL), BF16),
                vmem((2, SKEL, DIM), F32),
                vmem((3, 4, SKEL, DIM), F32),
                vmem((2, 2, CLS, SKEL), F32),
                vmem((6, 4, HALF, SKEL), F32),
                vmem((2, CLS, SKEL), F32),
                vmem((3, 2, CLS, 128), F32),
                vmem((9, 4, CLS, 128), F32),
                pltpu.SemaphoreType.DMA((26,)),
                pltpu.SemaphoreType.DMA((70,)),
                pltpu.SemaphoreType.DMA((70,)),
            ],
            compiler_params=pltpu.CompilerParams(
                collective_id=0, has_side_effects=True, vmem_limit_bytes=67043328
            ),
        )(points, right_side, neighbours, leaf_interp, leaf_skeleton, node_skeleton, node_gain, transfer)

    in_specs = (
        P("leaf", None), P(None, "leaf"), P("leaf", None), P("leaf", None, None),
        P("leaf", None), P(), P(), P(),
    )
    out_specs = (P(None, "leaf"), P(None, "leaf"))
    return jax.shard_map(device, mesh=mesh, in_specs=in_specs, out_specs=out_specs, check_vma=False)
```

time: 702 us -> 120 us (0.17); the launches traced: 689 us -> 120 us
  matrix products: 261 us -> 0 us
  blocking collectives: 153 us -> 0 us
  Pallas kernels: 0 us -> 115 us
  other arithmetic: 101 us -> 0 us
  local copies, waits for them, and re-layouts: 99.6 us -> 4.54 us
  starting transfers between devices: 52.6 us -> 0 us
  waiting for transfers between devices: 18 us -> 0 us
    dot_general x118 -> x0, matrix products: 260 us -> none  [the longest x10 94.2 us: body(): jnp.einsum('cnq,nqp->cnp', shifted, near_tiles[operate_slot_id], precisio...]
    psum x12 -> x0, blocking collectives: 153 us -> none  [over_axes(): return functools.reduce(lax.psum, axes, x)]
    pallas_call x0 -> x1, Pallas kernels: none -> 115 us  [device(): pl.pallas_call(body, out_shape=(out, out), in_specs=[any_space, any_space...]
    gather x10 -> x0, local copies, waits for them, and re-layouts: 56.5 us -> none  [the longest x3 25.4 us: body(): jnp.take_along_axis(paired.reshape(node_count // 2, 2 * skel_size, coord_...]
    ppermute x27 -> x0, starting transfers between devices: 52.6 us -> none  [the longest x21 39.2 us: swapped(): return lax.ppermute(block, axis, route)]
    another operation x19 -> x0, other arithmetic: 37.7 us -> none  [the longest x9 20.3 us: chol_apply(): factor = jnp.linalg.cholesky(matrix)]
    reduce_sum x15 -> x0, other arithmetic: 26 us -> none  [the longest x9 13.7 us: pair_kernel(): second_norm = jnp.sum(second_set * second_set, axis=-1)]
    select_n x20 -> x0, other arithmetic: 20.1 us -> none  [the longest x6 7.58 us: body(): jnp.take_along_axis(paired.reshape(node_count // 2, 2 * skel_size, coord_...]
  transfers between devices with their start and end apart: 27 -> 0, of which waited for: 7 -> 0; matrix products, arithmetic and copies ran while one was open for 48% -> 0% of each run, Pallas kernels for 0% -> 0%
where the time goes in v1:
time: 120 us
  Pallas kernels  115 us (96%)
  local copies, waits for them, and re-layouts  4.54 us (4%)
    pallas_call x1, Pallas kernels, device(): pl.pallas_call(body, out_shape=(out, out), in_specs=[any_space, any_space...  115 us
    unnamed x2, local copies, waits for them, and re-layouts  4.54 us

profile of v1, /device:TPU:0, one launch (start us, length us, event | category | flops | bytes accessed | tf_op | source)
XLA Modules:
  0.0 119.9 jit_solution(14175265361373473663)
XLA Ops:
  0.6 114.7 %shard_map.95 = (f32[64,4096]{1,0:T(8,128)}, f32[64,4096]{1,0:T(8,128)}) custom-call(f32[4096,128]{1,0:T(8,128)} %points.1, f32[64,4096]{1,0:T(8,128)} %right_side.1, s32[8,5]{1,0:T(8,128)} %neighbours.1, f32[8,512,256]{2,1,0:T(8,128)} %leaf_interp.1, s32[8,256]{1,0:T(8,128)} %leaf_skeleton.1, s32[1022,256]{1,0:T(8,128)} %node_skeleton.1, ...), custom_call_target="tpu_custom_call" | custom-call | tf_op jit(solution)/shard_map/pallas_call | solution.py:641
  115.4 2.3 %copy.12 = f32[64,4096]{1,0:T(8,128)} copy(f32[64,4096]{1,0:T(8,128)} %get-tuple-element.4) | data formatting | bytes 2097152
  117.6 2.3 %copy.13 = f32[64,4096]{1,0:T(8,128)} copy(f32[64,4096]{1,0:T(8,128)} %get-tuple-element.5) | data formatting | bytes 2097152

commit v2 on v1

--- a/solution.py
+++ b/solution.py
@@ -136,7 +136,6 @@
 
     own_rows = pl.ds(OWN, LV * LEAF)
     load_points = load(points, xe.at[own_rows, :])
-    load_b = load(right_side, be.at[:, own_rows])
     load_small = [load(leaf_skeleton, lsk)]
 
     def gain_row(level):
@@ -159,6 +158,7 @@
             load_small.append(load(node_skeleton.at[pl.ds(at, 8), :], nw.at[level]))
         else:
             load_small.append(load(node_skeleton.at[pl.ds(1016, 6), :], nw.at[level, pl.ds(0, 6), :]))
+    load_b = load(right_side, be.at[:, own_rows])
     load_itp = load(leaf_interp, itp)
     load_tra = load(transfer, tra)
 
@@ -166,7 +166,6 @@
     barrier = pltpu.get_barrier_semaphore()
     for other in peers:
         pl.semaphore_signal(barrier, inc=1, device_id=(other,), device_id_type=MESH)
-    pl.semaphore_wait(barrier, len(peers))
 
     sent = []
 
@@ -187,19 +186,22 @@
         for copy in copies:
             copy.wait_recv()
 
-    load_points.wait()
     first, last = pl.ds(OWN, OWN), pl.ds(OWN + (LV - 2) * LEAF, OWN)
     head, tail = pl.ds(0, OWN), pl.ds(OWN + LV * LEAF, OWN)
-    halo_x = [send(xe.at[first, :], xe.at[tail, :], left), send(xe.at[last, :], xe.at[head, :], right)]
-    load_b.wait()
-    halo_b = [send(be.at[:, first], be.at[:, tail], left), send(be.at[:, last], be.at[:, head], right)]
+
+    def halo_rows(ref):
+        return [send(ref.at[first, :], ref.at[tail, :], left), send(ref.at[last, :], ref.at[head, :], right)]
+
+    def halo_columns(ref):
+        return [send(ref.at[:, first], ref.at[:, tail], left), send(ref.at[:, last], ref.at[:, head], right)]
+
+    def split_rows(e):
+        rows = pl.ds(pl.multiple_of(e * LEAF, LEAF), LEAF)
+        xhl[rows, :] = jnp.concatenate(split(xe[rows, :]), axis=1)
 
     def prepare(e):
         rows = pl.ds(pl.multiple_of(e * LEAF, LEAF), LEAF)
-        x = xe[rows, :]
-        high, low = split(x)
-        xhl[rows, :] = jnp.concatenate([high, low], axis=1)
-        a, b = norm_columns(x)
+        a, b = norm_columns(xe[rows, :])
         n1[rows, :] = a
         n2[rows, :] = b
 
@@ -216,11 +218,8 @@
 
         lax.fori_loop(start, stop, step, 0)
 
-    def own_setup(e):
-        prepare(e)
-        split_columns(be, e)
-
-    loop(2, 10, own_setup)
+    load_points.wait()
+    loop(2, 10, split_rows)
 
     for copy in load_small:
         copy.wait()
@@ -270,25 +269,23 @@
         fl[slot] = low
 
     skel = [pick(j, xhl[pl.ds(OWN + j * LEAF, LEAF), :]) for j in range(LV)]
-    slot, index = 0, 8
+    index = 8
+    pairs = []
     while len(skel) > 1:
         parents = []
         for i in range(len(skel) // 2):
-            far_tile(slot, skel[2 * i + 1], skel[2 * i])
+            pairs.append((skel[2 * i + 1], skel[2 * i]))
             parents.append(pick(index, jnp.concatenate(skel[2 * i : 2 * i + 2], axis=0)))
-            slot += 1
             index += 1
         skel = parents
     skel3 = skel[0]
     s_r0[0] = joined(skel3)
+    pl.semaphore_wait(barrier, len(peers))
     copy_s = [send(s_r0.at[0], s_r0.at[1], partner)]
 
     def gain(level, node):
         row = node % 8
         return gw[level, pl.ds(row, 1), :]
-
-    load_itp.wait()
-    load_tra.wait()
 
     class Tree:
         pass
@@ -361,10 +358,25 @@
         u4[it, my_half, :] = pot
         t.copies = [send(u4.at[it, my_half, :], u4.at[it, my_half, :], partner)]
 
-    def down_local(it, t, store):
+    def down_device(it, t):
         arrive(t.copies)
         pot = times_f32(u4[it], tra[3, core], 1) * gain(3, me)
-        pot = pot + times(stack(w_r0[it, 1]), fh[7], fl[7])
+        t.top = pot + times(stack(w_r0[it, 1]), fh[7], fl[7])
+
+    def tree_gram(t):
+        total = None
+        slot = 0
+        for level in range(3):
+            rows = t.levels[level]
+            for i in range(len(rows) // 2):
+                part = times(stack(rows[2 * i + 1]), fh[slot], fl[slot])
+                part = times_f32(rows[2 * i], part, 1)
+                total = part if total is None else total + part
+                slot += 1
+        return total
+
+    def down_local(it, t, store):
+        pot = t.top
         slot = 7
         for level in (2, 1, 0):
             rows = t.levels[level]
@@ -385,26 +397,40 @@
             high, low = split(itp[j])
             store(j, times(stack(pot[j * CLS : (j + 1) * CLS]), high, low, 1))
 
+    my_points = pl.ds(pl.multiple_of(core * 128, 128), 128)
+
+    def send_skel(q):
+        return [
+            send(s_q.at[q, 0, my_points, :], s_q.at[q, s, my_points, :], peer(q, s)) for s in (1, 2, 3)
+        ]
+
+    def forward_skel(q, copies):
+        arrive(copies)
+        part = s_q.at[q, pl.ds(1, 3), my_points, :]
+        return [send(part, part, partner)]
+
     def skel_core():
         arrive(copy_s)
         other = jnp.concatenate(split(s_r0[1]), axis=1)
-        far_tile(7, other, skel3)
         own = pick(15, jnp.concatenate([skel3, other], axis=0))
         s_q[0, 0] = joined(own)
-        return own, send_quad(s_q, 0, 0)
+        return (own, [(7, other, skel3)], send_skel(0))
 
     def skel_quad(q, own, copies):
         arrive(copies)
         s1, s2, s3 = [jnp.concatenate(split(s_q[q, s]), axis=1) for s in (1, 2, 3)]
-        far_tile(8 + 2 * q, s1, own)
         mine = pick(16 + 3 * q, jnp.concatenate([own, s1], axis=0))
         theirs = pick(17 + 3 * q, jnp.concatenate([s2, s3], axis=0))
-        far_tile(9 + 2 * q, theirs, mine)
+        tiles = [(8 + 2 * q, s1, own), (9 + 2 * q, theirs, mine)]
         if q == 2:
-            return None, None
+            return None, tiles, None
         up = pick(18 + 3 * q, jnp.concatenate([mine, theirs], axis=0))
         s_q[q + 1, 0] = joined(up)
-        return up, send_quad(s_q, q + 1, q + 1)
+        return up, tiles, send_skel(q + 1)
+
+    def far_tiles(tiles):
+        for tile in tiles:
+            far_tile(*tile)
 
     def build(t):
         e = (t + 6) // 3
@@ -480,94 +506,118 @@
     def unfolded(m):
         return jnp.concatenate([m[:, :CLS], m[:, CLS:]], axis=0)
 
+    def square_t(m):
+        return jnp.concatenate([m, jnp.zeros_like(m)], axis=1)
+
+    def low_pairs_t(m):
+        return transposed(square_t(m))[:CLS, :CLS]
+
+    loop(2, 10, prepare)
+    far_tiles([(i, *pair) for i, pair in enumerate(pairs)])
+    loop(0, 2, build)
+    own4, tiles3, copy_s = skel_core()
+    load_b.wait()
+
+    def split_b(e):
+        split_columns(be, e)
+
+    loop(2, 10, split_b)
+    load_itp.wait()
+    load_tra.wait()
     t0 = up_local(0)
     sum0 = sum_start(0, folded(gram([(be, OWN, be, OWN)])[0]))
-    loop(0, 5, build)
+    loop(2, 5, build)
     up_core(0, t0)
-    own4, copy_s = skel_core()
     sum_step(sum0, 0)
-    loop(5, 10, build)
+    far_tiles(tiles3)
+    loop(5, 9, build)
+    copy_s = forward_skel(0, copy_s)
+    halo_x = halo_rows(xe)
+    halo_b = halo_columns(be)
+    loop(9, 11, build)
+    own6, tiles4, copy_s = skel_quad(0, own4, copy_s)
+    loop(11, 13, build)
     up_quad(0, t0, 0)
-    own6, copy_s = skel_quad(0, own4, copy_s)
     sum_step(sum0, 1)
-    loop(10, 15, build)
+    far_tiles(tiles4)
+    loop(13, 20, build)
+    copy_s = forward_skel(1, copy_s)
     up_quad(0, t0, 1)
-    own8, copy_s = skel_quad(1, own6, copy_s)
     sum_step(sum0, 2)
-    loop(15, 20, build)
-    up_quad(0, t0, 2)
-    skel_quad(2, own8, copy_s)
-    m0 = unfolded(sum_step(sum0, 3))
-    down_top(0, t0)
+    own8, tiles6, copy_s = skel_quad(1, own6, copy_s)
+    far_tiles(tiles6)
     arrive(halo_x)
 
     def halo_setup(e):
+        split_rows(e)
         prepare(e)
 
     loop(0, 2, halo_setup)
     loop(10, 12, halo_setup)
     loop(20, 24, build)
+    arrive(halo_b)
+    copy_s = forward_skel(2, copy_s)
     for t in (-4, -2, -1):
         build(t)
+    loop(0, 2, split_b)
+    loop(10, 12, split_b)
+    up_quad(0, t0, 2)
+    m0 = unfolded(sum_step(sum0, 3))
+    _, tiles8, _ = skel_quad(2, own8, copy_s)
+    far_tiles(tiles8)
+    down_top(0, t0)
+
+    def first_near(j):
+        cols = pl.ds(pl.multiple_of((j + 2) * LEAF, LEAF), LEAF)
+        ye[:, cols] = be[:, cols] + near_target(ye, j)
+
+    loop(0, LV, first_near)
+    down_device(0, t0)
 
     def store_first(j, far):
         cols = pl.ds(OWN + j * LEAF, LEAF)
-        ye[:, cols] = far + be[:, cols]
+        ye[:, cols] = ye[:, cols] + far
 
     down_local(0, t0, store_first)
-    arrive(halo_b)
-
-    def split_b(e):
-        split_columns(be, e)
-
-    loop(0, 2, split_b)
-    loop(10, 12, split_b)
-
-    def first_near(j):
-        cols = pl.ds(pl.multiple_of((j + 2) * LEAF, LEAF), LEAF)
-        ye[:, cols] = ye[:, cols] + near_target(ye, j)
-
-    loop(0, LV, first_near)
-
-    halo_y = [send(ye.at[:, first], ye.at[:, tail], left), send(ye.at[:, last], ye.at[:, head], right)]
 
     def split_y(e):
         split_columns(ye, e)
 
     loop(2, 10, split_y)
     t1 = up_local(1)
+    halo_y = halo_columns(ye)
     sum1 = sum_start(1, jnp.concatenate(gram([(be, OWN, ye, OWN), (ye, OWN, ye, OWN)]), axis=1))
 
     def second_near(j):
         cols = pl.ds(pl.multiple_of(j * LEAF, LEAF), LEAF)
         near[:, cols] = near_target(near, j)
 
-    loop(2, 4, second_near)
     up_core(1, t1)
     sum_step(sum1, 0)
-    loop(4, 5, second_near)
+    low_pairs = tree_gram(t1)
+    loop(2, 6, second_near)
     up_quad(1, t1, 0)
     sum_step(sum1, 1)
-    loop(5, 6, second_near)
-    up_quad(1, t1, 1)
-    sum_step(sum1, 2)
     arrive(halo_y)
     loop(0, 2, split_y)
     loop(10, 12, split_y)
     loop(0, 2, second_near)
+    loop(6, 8, second_near)
+    up_quad(1, t1, 1)
+    sum_step(sum1, 2)
+    near_gram = gram([(ye, OWN, near, 0)])[0]
     up_quad(1, t1, 2)
     down_top(1, t1)
     moments = sum_step(sum1, 3)
-    loop(6, 8, second_near)
+    down_device(1, t1)
+    bends = near_gram + low_pairs + low_pairs_t(low_pairs) + times_f32(w_r0[1, 0], t1.top, 1)
+    curve = sum_start(2, folded(bends))
 
     def store_second(j, far):
         cols = pl.ds(j * LEAF, LEAF)
         near[:, cols] = near[:, cols] + far + ye[:, pl.ds(OWN + j * LEAF, LEAF)]
 
     down_local(1, t1, store_second)
-
-    def square_t(m):
-        return jnp.concatenate([m, jnp.zeros_like(m)], axis=1)
 
     def sym(m):
         return 0.5 * (m + transposed(square_t(m))[:CLS, :CLS])
@@ -598,8 +648,11 @@
         dirn[:, cols] = mix(plus_s, be[:, wide]) - mix(alpha_s, ye[:, wide])
         near[:, cols] = mix(plus_s, ye[:, wide]) - mix(alpha_s, near[:, cols])
 
+    sum_step(curve, 0)
     loop(0, LV, make_second)
-    curve = sum_start(2, folded(gram([(dirn, 0, near, 0)])[0]))
+    sum_step(curve, 1)
+    for copy in halo_b + halo_y:
+        copy.wait_send()
 
     def first_update(j):
         wide = pl.ds(pl.multiple_of((j + 2) * LEAF, LEAF), LEAF)
@@ -607,13 +660,13 @@
         be[:, wide] = mix(alpha_s, old)
         ye[:, wide] = old - mix(alpha_s, ye[:, wide])
 
-    sum_step(curve, 0)
-    for copy in halo_b + halo_y:
-        copy.wait_send()
     loop(0, LV, first_update)
-    sum_step(curve, 1)
+    plus = transposed(square_t(plus_t))[:CLS, :CLS]
+    known = times_f32(times_f32(plus_t, m1), plus) - 2.0 * sym(times_f32(times_f32(plus_t, m2), alpha))
+    known = known + times_f32(times_f32(alpha_t, m2), alpha)
     sum_step(curve, 2)
-    curvature = sym(unfolded(sum_step(curve, 3)))
+    bends = unfolded(sum_step(curve, 3))
+    curvature = sym(known + times_f32(times_f32(alpha_t, bends), alpha))
     last_t = transposed(solve(curvature, new))[CLS:, :CLS]
     last_s = stack(last_t)
 
@@ -675,8 +728,8 @@
                 vmem((3, 2, CLS, 128), F32),
                 vmem((9, 4, CLS, 128), F32),
                 pltpu.SemaphoreType.DMA((26,)),
-                pltpu.SemaphoreType.DMA((70,)),
-                pltpu.SemaphoreType.DMA((70,)),
+                pltpu.SemaphoreType.DMA((72,)),
+                pltpu.SemaphoreType.DMA((72,)),
             ],
             compiler_params=pltpu.CompilerParams(
                 collective_id=0, has_side_effects=True, vmem_limit_bytes=67043328

time: 120 us -> 115 us (0.958)
  Pallas kernels: 115 us -> 109 us
    pallas_call x1, Pallas kernels: 115 us -> 109 us  [device(): pl.pallas_call(body, out_shape=(out, out), in_specs=[any_space, any_space...]
where the time goes in v2:
time: 115 us
  Pallas kernels  109 us (95%)
  local copies, waits for them, and re-layouts  4.54 us (4%)
    pallas_call x1, Pallas kernels, device(): pl.pallas_call(body, out_shape=(out, out), in_specs=[any_space, any_space...  109 us
    unnamed x2, local copies, waits for them, and re-layouts  4.54 us

profile of v2, /device:TPU:0, one launch (start us, length us, event | category | flops | bytes accessed | tf_op | source)
XLA Modules:
  0.0 114.6 jit_solution(2636796079870373201)
XLA Ops:
  0.6 109.4 %shard_map.95 = (f32[64,4096]{1,0:T(8,128)}, f32[64,4096]{1,0:T(8,128)}) custom-call(f32[4096,128]{1,0:T(8,128)} %points.1, f32[64,4096]{1,0:T(8,128)} %right_side.1, s32[8,5]{1,0:T(8,128)} %neighbours.1, f32[8,512,256]{2,1,0:T(8,128)} %leaf_interp.1, s32[8,256]{1,0:T(8,128)} %leaf_skeleton.1, s32[1022,256]{1,0:T(8,128)} %node_skeleton.1, ...), custom_call_target="tpu_custom_call" | custom-call | tf_op jit(solution)/shard_map/pallas_call | solution.py:694
  110.1 2.3 %copy.12 = f32[64,4096]{1,0:T(8,128)} copy(f32[64,4096]{1,0:T(8,128)} %get-tuple-element.4) | data formatting | bytes 2097152
  112.3 2.3 %copy.13 = f32[64,4096]{1,0:T(8,128)} copy(f32[64,4096]{1,0:T(8,128)} %get-tuple-element.5) | data formatting | bytes 2097152

commit v3 on v2

--- a/solution.py
+++ b/solution.py
@@ -96,9 +96,9 @@
 
 def body(
     points, right_side, neighbours, leaf_interp, leaf_skeleton, node_skeleton, node_gain, transfer,
-    x_out, r_out,
+    x_out, r_out, d_out, a_out, c_out,
     xe, xhl, n1, n2, tile_h, tile_l, be, ye, near, dirn, vs, itp, tra, gw, nw, lsk, idx_rows, idx_cols,
-    fh, fl, s_r0, s_q, w_r0, w_q, u4, ar_r0, ar_q,
+    fh, fl, s_r0, s_q, w_r0, w_q, u4, ar_r0, ar_q, coef,
     local_sem, send_sem, recv_sem,
 ):
     me = lax.axis_index("leaf")
@@ -220,6 +220,14 @@
 
     load_points.wait()
     loop(2, 10, split_rows)
+
+    def loop2(start, stop, f):
+        def step(i, carry):
+            f(start + 2 * i)
+            f(start + 2 * i + 1)
+            return carry
+
+        lax.fori_loop(0, (stop - start) // 2, step, 0)
 
     for copy in load_small:
         copy.wait()
@@ -282,6 +290,7 @@
     s_r0[0] = joined(skel3)
     pl.semaphore_wait(barrier, len(peers))
     copy_s = [send(s_r0.at[0], s_r0.at[1], partner)]
+    halo_x = halo_rows(xe)
 
     def gain(level, node):
         row = node % 8
@@ -446,14 +455,21 @@
         tile_h[t + 4] = high
         tile_l[t + 4] = low
 
-    def near_target(out, j):
+    def near_target(j):
         total = None
-        for o in (0, -1, -2, 1, 2):
+        for o in (0, -1, -2):
             cols = pl.ds(pl.multiple_of((j + 2 + o) * LEAF, LEAF), LEAF)
-            t = 3 * j + o if o >= 0 else 3 * (j + o) - o
-            part = times(vs[:, cols], tile_h[t + 4], tile_l[t + 4], 1 if o > 0 else 0)
+            t = 3 * (j + o) - o
+            part = times(vs[:, cols], tile_h[t + 4], tile_l[t + 4])
             total = part if total is None else total + part
-        return total
+        turned = None
+        for o in (1, 2):
+            cols = pl.ds(pl.multiple_of((j + 2 + o) * LEAF, LEAF), LEAF)
+            t = 3 * j + o
+            part = dot(tile_h[t + 4], vs[:, cols], 1, 1) + dot(tile_l[t + 4], vs[:, cols], 1, 1)
+            turned = part if turned is None else turned + part
+        turned = turned.T
+        return total + (turned[:CLS] + turned[CLS:])
 
     def gram(pairs):
         sums = None
@@ -512,9 +528,17 @@
     def low_pairs_t(m):
         return transposed(square_t(m))[:CLS, :CLS]
 
-    loop(2, 10, prepare)
+    def sym(m):
+        return 0.5 * (m + transposed(square_t(m))[:CLS, :CLS])
+
+    def inverse_of(m):
+        row = lax.broadcasted_iota(I32, (CLS, CLS), 0)
+        col = lax.broadcasted_iota(I32, (CLS, CLS), 1)
+        return solve(m, jnp.where(row == col, 1.0, 0.0).astype(F32))[:, CLS:]
+
+    loop2(2, 10, prepare)
     far_tiles([(i, *pair) for i, pair in enumerate(pairs)])
-    loop(0, 2, build)
+    loop2(0, 2, build)
     own4, tiles3, copy_s = skel_core()
     load_b.wait()
 
@@ -526,25 +550,23 @@
     load_tra.wait()
     t0 = up_local(0)
     sum0 = sum_start(0, folded(gram([(be, OWN, be, OWN)])[0]))
-    loop(2, 5, build)
+    loop2(2, 6, build)
     up_core(0, t0)
     sum_step(sum0, 0)
     far_tiles(tiles3)
-    loop(5, 9, build)
+    loop2(6, 10, build)
     copy_s = forward_skel(0, copy_s)
-    halo_x = halo_rows(xe)
-    halo_b = halo_columns(be)
-    loop(9, 11, build)
+    loop2(10, 12, build)
     own6, tiles4, copy_s = skel_quad(0, own4, copy_s)
-    loop(11, 13, build)
     up_quad(0, t0, 0)
     sum_step(sum0, 1)
     far_tiles(tiles4)
-    loop(13, 20, build)
+    loop2(12, 20, build)
     copy_s = forward_skel(1, copy_s)
     up_quad(0, t0, 1)
     sum_step(sum0, 2)
     own8, tiles6, copy_s = skel_quad(1, own6, copy_s)
+    halo_b = halo_columns(be)
     far_tiles(tiles6)
     arrive(halo_x)
 
@@ -554,9 +576,9 @@
 
     loop(0, 2, halo_setup)
     loop(10, 12, halo_setup)
-    loop(20, 24, build)
+    loop2(20, 24, build)
+    copy_s = forward_skel(2, copy_s)
     arrive(halo_b)
-    copy_s = forward_skel(2, copy_s)
     for t in (-4, -2, -1):
         build(t)
     loop(0, 2, split_b)
@@ -569,9 +591,9 @@
 
     def first_near(j):
         cols = pl.ds(pl.multiple_of((j + 2) * LEAF, LEAF), LEAF)
-        ye[:, cols] = be[:, cols] + near_target(ye, j)
-
-    loop(0, LV, first_near)
+        ye[:, cols] = be[:, cols] + near_target(j)
+
+    loop2(0, LV, first_near)
     down_device(0, t0)
 
     def store_first(j, far):
@@ -585,26 +607,27 @@
 
     loop(2, 10, split_y)
     t1 = up_local(1)
-    halo_y = halo_columns(ye)
     sum1 = sum_start(1, jnp.concatenate(gram([(be, OWN, ye, OWN), (ye, OWN, ye, OWN)]), axis=1))
 
     def second_near(j):
         cols = pl.ds(pl.multiple_of(j * LEAF, LEAF), LEAF)
-        near[:, cols] = near_target(near, j)
+        near[:, cols] = near_target(j)
 
     up_core(1, t1)
     sum_step(sum1, 0)
     low_pairs = tree_gram(t1)
-    loop(2, 6, second_near)
+    loop2(2, 6, second_near)
     up_quad(1, t1, 0)
     sum_step(sum1, 1)
+    halo_y = halo_columns(ye)
+    inverse0 = inverse_of(sym(m0))
+    up_quad(1, t1, 1)
+    sum_step(sum1, 2)
     arrive(halo_y)
     loop(0, 2, split_y)
     loop(10, 12, split_y)
-    loop(0, 2, second_near)
-    loop(6, 8, second_near)
-    up_quad(1, t1, 1)
-    sum_step(sum1, 2)
+    loop2(0, 2, second_near)
+    loop2(6, 8, second_near)
     near_gram = gram([(ye, OWN, near, 0)])[0]
     up_quad(1, t1, 2)
     down_top(1, t1)
@@ -617,23 +640,24 @@
         cols = pl.ds(j * LEAF, LEAF)
         near[:, cols] = near[:, cols] + far + ye[:, pl.ds(OWN + j * LEAF, LEAF)]
 
-    down_local(1, t1, store_second)
-
-    def sym(m):
-        return 0.5 * (m + transposed(square_t(m))[:CLS, :CLS])
-
     m0 = sym(m0)
     m1 = moments[:, :CLS]
     m2 = moments[:, CLS:]
     step = solve(sym(m1), m0)
+    sum_step(curve, 0)
     alpha = step[:, CLS:]
     alpha_t = transposed(step)[CLS:, :CLS]
     cross = times_f32(m1, alpha)
     new = m0 - 2.0 * sym(cross) + sym(times_f32(times_f32(alpha_t, m2), alpha))
-    beta_t = transposed(solve(m0, new))[CLS:, :CLS]
+    beta = times_f32(inverse0, new)
+    beta_t = low_pairs_t(beta)
     row = lax.broadcasted_iota(I32, (CLS, CLS), 0)
     col = lax.broadcasted_iota(I32, (CLS, CLS), 1)
-    plus_t = jnp.where(row == col, 1.0, 0.0) + beta_t
+    unit = jnp.where(row == col, 1.0, 0.0)
+    plus = unit + beta
+    plus_t = unit + beta_t
+    down_local(1, t1, store_second)
+    sum_step(curve, 1)
 
     alpha_s = stack(alpha_t)
     plus_s = stack(plus_t)
@@ -642,42 +666,31 @@
         high, low = split(x)
         return times(matrix_s, high, low)
 
-    def make_second(j):
-        cols = pl.ds(pl.multiple_of(j * LEAF, LEAF), LEAF)
-        wide = pl.ds(pl.multiple_of((j + 2) * LEAF, LEAF), LEAF)
-        dirn[:, cols] = mix(plus_s, be[:, wide]) - mix(alpha_s, ye[:, wide])
-        near[:, cols] = mix(plus_s, ye[:, wide]) - mix(alpha_s, near[:, cols])
-
-    sum_step(curve, 0)
-    loop(0, LV, make_second)
-    sum_step(curve, 1)
     for copy in halo_b + halo_y:
         copy.wait_send()
 
-    def first_update(j):
-        wide = pl.ds(pl.multiple_of((j + 2) * LEAF, LEAF), LEAF)
-        old = be[:, wide]
+    def update(j):
+        cols = pl.ds(pl.multiple_of(j * 2 * LEAF, LEAF), 2 * LEAF)
+        wide = pl.ds(pl.multiple_of((j + 1) * 2 * LEAF, LEAF), 2 * LEAF)
+        old, image = be[:, wide], ye[:, wide]
+        start = mix(alpha_s, image)
+        dirn[:, cols] = mix(plus_s, old) - start
+        near[:, cols] = mix(plus_s, image) - mix(alpha_s, near[:, cols])
         be[:, wide] = mix(alpha_s, old)
-        ye[:, wide] = old - mix(alpha_s, ye[:, wide])
-
-    loop(0, LV, first_update)
-    plus = transposed(square_t(plus_t))[:CLS, :CLS]
+        ye[:, wide] = old - start
+
+    loop(0, LV // 2, update)
+    outs = [
+        load(be.at[:, own_rows], x_out), load(ye.at[:, own_rows], r_out),
+        load(dirn, d_out), load(near, a_out),
+    ]
+    sum_step(curve, 2)
     known = times_f32(times_f32(plus_t, m1), plus) - 2.0 * sym(times_f32(times_f32(plus_t, m2), alpha))
     known = known + times_f32(times_f32(alpha_t, m2), alpha)
-    sum_step(curve, 2)
     bends = unfolded(sum_step(curve, 3))
     curvature = sym(known + times_f32(times_f32(alpha_t, bends), alpha))
-    last_t = transposed(solve(curvature, new))[CLS:, :CLS]
-    last_s = stack(last_t)
-
-    def last_update(j):
-        cols = pl.ds(pl.multiple_of(j * LEAF, LEAF), LEAF)
-        wide = pl.ds(pl.multiple_of((j + 2) * LEAF, LEAF), LEAF)
-        be[:, wide] = be[:, wide] + mix(last_s, dirn[:, cols])
-        ye[:, wide] = ye[:, wide] - mix(last_s, near[:, cols])
-
-    loop(0, LV, last_update)
-    outs = [load(be.at[:, own_rows], x_out), load(ye.at[:, own_rows], r_out)]
+    coef[...] = transposed(solve(curvature, new))[CLS:, :]
+    outs.append(load(coef, c_out))
     for copy in outs:
         copy.wait()
     for copy in sent:
@@ -685,20 +698,28 @@
             copy.wait_send()
 
 
+def finish(coef, x0, r1, direction, image, x_out, r_out):
+    last_s = stack(coef[:, :CLS])
+    high, low = split(direction[...])
+    x_out[...] = x0[...] + times(last_s, high, low)
+    high, low = split(image[...])
+    r_out[...] = r1[...] - times(last_s, high, low)
+
+
 def solution(mesh):
     any_space = pl.BlockSpec(memory_space=pl.ANY)
     vmem = pltpu.VMEM
 
     def device(points, right_side, neighbours, leaf_interp, leaf_skeleton, node_skeleton, node_gain, transfer):
         out = jax.ShapeDtypeStruct(right_side.shape, F32)
-        return pl.pallas_call(
+        x0, r1, direction, image, coef = pl.pallas_call(
             body,
-            out_shape=(out, out),
+            out_shape=(out, out, out, out, jax.ShapeDtypeStruct((CLS, 128), F32)),
             in_specs=[
                 any_space, any_space, pl.BlockSpec(memory_space=pltpu.SMEM), any_space,
                 any_space, any_space, any_space, any_space,
             ],
-            out_specs=(any_space, any_space),
+            out_specs=(any_space,) * 5,
             scratch_shapes=[
                 vmem((WIDE, DIM), F32),
                 vmem((WIDE, 2 * DIM), BF16),
@@ -727,7 +748,8 @@
                 vmem((2, CLS, SKEL), F32),
                 vmem((3, 2, CLS, 128), F32),
                 vmem((9, 4, CLS, 128), F32),
-                pltpu.SemaphoreType.DMA((26,)),
+                vmem((CLS, 128), F32),
+                pltpu.SemaphoreType.DMA((28,)),
                 pltpu.SemaphoreType.DMA((72,)),
                 pltpu.SemaphoreType.DMA((72,)),
             ],
@@ -735,6 +757,14 @@
                 collective_id=0, has_side_effects=True, vmem_limit_bytes=67043328
             ),
         )(points, right_side, neighbours, leaf_interp, leaf_skeleton, node_skeleton, node_gain, transfer)
+        block = pl.BlockSpec((CLS, 2 * LEAF), lambda j: (0, j))
+        return pl.pallas_call(
+            finish,
+            grid=(LV // 2,),
+            out_shape=(out, out),
+            in_specs=[pl.BlockSpec((CLS, 128), lambda j: (0, 0)), block, block, block, block],
+            out_specs=(block, block),
+        )(coef, x0, r1, direction, image)
 
     in_specs = (
         P("leaf", None), P(None, "leaf"), P("leaf", None), P("leaf", None, None),

time: 115 us -> 109 us (0.948)
  local copies, waits for them, and re-layouts: 4.54 us -> 0 us
    unnamed x2 -> x0, local copies, waits for them, and re-layouts: 4.54 us -> none
    pallas_call x1 -> x2, Pallas kernels: 109 us -> 108 us  [the longest x1 103 us: device(): pl.pallas_call(body, out_shape=(out, out, out, out, jax.ShapeDtypeStruct(...]
where the time goes in v3:
time: 109 us
  Pallas kernels  108 us (99%)
    pallas_call x1, Pallas kernels, device(): pl.pallas_call(body, out_shape=(out, out, out, out, jax.ShapeDtypeStruct(...  103 us
    pallas_call x1, Pallas kernels, device(): pl.pallas_call(finish, grid=(LV // 2,), out_shape=(out, out), in_specs=[p...  4.57 us

profile of v3, /device:TPU:0, one launch (start us, length us, event | category | flops | bytes accessed | tf_op | source)
XLA Modules:
  0.0 108.5 jit_solution(3941137009637625612)
XLA Ops:
  0.6 103.3 %shard_map.95 = (f32[64,4096]{1,0:T(8,128)}, f32[64,4096]{1,0:T(8,128)}, f32[64,4096]{1,0:T(8,128)}, f32[64,4096]{1,0:T(8,128)}, f32[64,128]{1,0:T(8,128)}) custom-call(f32[4096,128]{1,0:T(8,128)} %points.1, f32[64,4096]{1,0:T(8,128)} %right_side.1, s32[8,5]{1,0:T(8,128)} %neighbours.1, f32[8,512,256]{2,1,0:T(8,128)} %leaf_interp.1, s32[8,256]{1,0:T(8,128)} %leaf_skeleton.1, ...), custom_call_target="tpu_custom_call" | custom-call | tf_op jit(solution)/shard_map/pallas_call | solution.py:715
  103.9 4.6 %shard_map.96 = (f32[64,4096]{1,0:T(8,128)}, f32[64,4096]{1,0:T(8,128)}) custom-call(f32[64,128]{1,0:T(8,128)} %get-tuple-element.7.coef, f32[64,4096]{1,0:T(8,128)} %get-tuple-element.8.x0, f32[64,4096]{1,0:T(8,128)} %get-tuple-element.9.r1, f32[64,4096]{1,0:T(8,128)} %get-tuple-element.10.direction, f32[64,4096]{1,0:T(8,128)} %get-tuple-element.11.image), custom_call_target="tpu_custom_call" | custom-call | tf_op jit(solution)/shard_map/pallas_call | solution.py:761

commit v4 on v3

--- a/solution.py
+++ b/solution.py
@@ -97,7 +97,7 @@
 def body(
     points, right_side, neighbours, leaf_interp, leaf_skeleton, node_skeleton, node_gain, transfer,
     x_out, r_out, d_out, a_out, c_out,
-    xe, xhl, n1, n2, tile_h, tile_l, be, ye, near, dirn, vs, itp, tra, gw, nw, lsk, idx_rows, idx_cols,
+    xe, xhl, n1, n2, tile_h, tile_l, be, ye, near, vs, itp, tra, gw, nw, lsk, idx_rows, idx_cols,
     fh, fl, s_r0, s_q, w_r0, w_q, u4, ar_r0, ar_q, coef,
     local_sem, send_sem, recv_sem,
 ):
@@ -219,6 +219,8 @@
         lax.fori_loop(start, stop, step, 0)
 
     load_points.wait()
+    pl.semaphore_wait(barrier, len(peers))
+    halo_x = halo_rows(xe)
     loop(2, 10, split_rows)
 
     def loop2(start, stop, f):
@@ -288,9 +290,7 @@
         skel = parents
     skel3 = skel[0]
     s_r0[0] = joined(skel3)
-    pl.semaphore_wait(barrier, len(peers))
     copy_s = [send(s_r0.at[0], s_r0.at[1], partner)]
-    halo_x = halo_rows(xe)
 
     def gain(level, node):
         row = node % 8
@@ -441,19 +441,16 @@
         for tile in tiles:
             far_tile(*tile)
 
-    def build(t):
-        e = (t + 6) // 3
-        k = (t + 6) % 3
+    def build_pair(e, k, flag):
         rows = pl.ds(pl.multiple_of(e * LEAF, LEAF), LEAF)
         cols = pl.ds(pl.multiple_of((e + k) * LEAF, LEAF), LEAF)
-        if isinstance(t, int):
-            flag = neighbours[e - 2, 2 + k] if e >= 2 else neighbours[e + k - 2, 2 - k]
-        else:
-            flag = neighbours[e - 2, 2 + k]
         mask = jnp.where(flag >= 0, 1.0, 0.0).astype(F32)
         high, low = split(jnp.exp(exponent(xhl[rows, :], n1[rows, :], xhl[cols, :], n2[cols, :])) * mask)
-        tile_h[t + 4] = high
-        tile_l[t + 4] = low
+        tile_h[3 * e + k - 2] = high
+        tile_l[3 * e + k - 2] = low
+
+    def build(t):
+        build_pair(t // 3 + 2, t % 3, neighbours[t // 3, 2 + t % 3])
 
     def near_target(j):
         total = None
@@ -538,7 +535,7 @@
 
     loop2(2, 10, prepare)
     far_tiles([(i, *pair) for i, pair in enumerate(pairs)])
-    loop2(0, 2, build)
+    loop(0, 2, build)
     own4, tiles3, copy_s = skel_core()
     load_b.wait()
 
@@ -554,46 +551,49 @@
     up_core(0, t0)
     sum_step(sum0, 0)
     far_tiles(tiles3)
-    loop2(6, 10, build)
+    loop2(6, 12, build)
     copy_s = forward_skel(0, copy_s)
-    loop2(10, 12, build)
-    own6, tiles4, copy_s = skel_quad(0, own4, copy_s)
     up_quad(0, t0, 0)
     sum_step(sum0, 1)
+    own6, tiles4, copy_s = skel_quad(0, own4, copy_s)
     far_tiles(tiles4)
     loop2(12, 20, build)
     copy_s = forward_skel(1, copy_s)
     up_quad(0, t0, 1)
     sum_step(sum0, 2)
     own8, tiles6, copy_s = skel_quad(1, own6, copy_s)
+    far_tiles(tiles6)
+
+    def first_near(j):
+        cols = pl.ds(pl.multiple_of((j + 2) * LEAF, LEAF), LEAF)
+        ye[:, cols] = be[:, cols] + near_target(j)
+
+    def at_halo(f):
+        return lambda i: f(i + 8 * (i // 2))
+
+    def at_edge(f):
+        return lambda i: f(i + 4 * (i // 2))
+
+    loop2(2, 6, first_near)
+    copy_s = forward_skel(2, copy_s)
+    up_quad(0, t0, 2)
+    m0 = unfolded(sum_step(sum0, 3))
+    _, tiles8, _ = skel_quad(2, own8, copy_s)
     halo_b = halo_columns(be)
-    far_tiles(tiles6)
+    far_tiles(tiles8)
+    down_top(0, t0)
     arrive(halo_x)
 
     def halo_setup(e):
         split_rows(e)
         prepare(e)
 
-    loop(0, 2, halo_setup)
-    loop(10, 12, halo_setup)
-    loop2(20, 24, build)
-    copy_s = forward_skel(2, copy_s)
+    loop(0, 4, at_halo(halo_setup))
+    loop(20, 24, build)
+    loop(0, 3, lambda i: build_pair((i + 1) // 2, 2 - i % 2, neighbours[i // 2, i % 2]))
     arrive(halo_b)
-    for t in (-4, -2, -1):
-        build(t)
-    loop(0, 2, split_b)
-    loop(10, 12, split_b)
-    up_quad(0, t0, 2)
-    m0 = unfolded(sum_step(sum0, 3))
-    _, tiles8, _ = skel_quad(2, own8, copy_s)
-    far_tiles(tiles8)
-    down_top(0, t0)
-
-    def first_near(j):
-        cols = pl.ds(pl.multiple_of((j + 2) * LEAF, LEAF), LEAF)
-        ye[:, cols] = be[:, cols] + near_target(j)
-
-    loop2(0, LV, first_near)
+    loop(0, 4, at_halo(split_b))
+    loop2(0, 4, at_edge(first_near))
     down_device(0, t0)
 
     def store_first(j, far):
@@ -605,6 +605,7 @@
     def split_y(e):
         split_columns(ye, e)
 
+    halo_y = halo_columns(ye)
     loop(2, 10, split_y)
     t1 = up_local(1)
     sum1 = sum_start(1, jnp.concatenate(gram([(be, OWN, ye, OWN), (ye, OWN, ye, OWN)]), axis=1))
@@ -616,18 +617,16 @@
     up_core(1, t1)
     sum_step(sum1, 0)
     low_pairs = tree_gram(t1)
-    loop2(2, 6, second_near)
+    loop2(2, 4, second_near)
     up_quad(1, t1, 0)
     sum_step(sum1, 1)
-    halo_y = halo_columns(ye)
+    loop2(4, 6, second_near)
     inverse0 = inverse_of(sym(m0))
     up_quad(1, t1, 1)
     sum_step(sum1, 2)
     arrive(halo_y)
-    loop(0, 2, split_y)
-    loop(10, 12, split_y)
-    loop2(0, 2, second_near)
-    loop2(6, 8, second_near)
+    loop(0, 4, at_halo(split_y))
+    loop2(0, 4, at_edge(second_near))
     near_gram = gram([(ye, OWN, near, 0)])[0]
     up_quad(1, t1, 2)
     down_top(1, t1)
@@ -643,8 +642,8 @@
     m0 = sym(m0)
     m1 = moments[:, :CLS]
     m2 = moments[:, CLS:]
+    sum_step(curve, 0)
     step = solve(sym(m1), m0)
-    sum_step(curve, 0)
     alpha = step[:, CLS:]
     alpha_t = transposed(step)[CLS:, :CLS]
     cross = times_f32(m1, alpha)
@@ -656,8 +655,9 @@
     unit = jnp.where(row == col, 1.0, 0.0)
     plus = unit + beta
     plus_t = unit + beta_t
+    sum_step(curve, 1)
     down_local(1, t1, store_second)
-    sum_step(curve, 1)
+    sum_step(curve, 2)
 
     alpha_s = stack(alpha_t)
     plus_s = stack(plus_t)
@@ -674,7 +674,9 @@
         wide = pl.ds(pl.multiple_of((j + 1) * 2 * LEAF, LEAF), 2 * LEAF)
         old, image = be[:, wide], ye[:, wide]
         start = mix(alpha_s, image)
-        dirn[:, cols] = mix(plus_s, old) - start
+        high, low = split(mix(plus_s, old) - start)
+        vs[pl.ds(0, CLS), wide] = high
+        vs[pl.ds(CLS, CLS), wide] = low
         near[:, cols] = mix(plus_s, image) - mix(alpha_s, near[:, cols])
         be[:, wide] = mix(alpha_s, old)
         ye[:, wide] = old - start
@@ -682,9 +684,8 @@
     loop(0, LV // 2, update)
     outs = [
         load(be.at[:, own_rows], x_out), load(ye.at[:, own_rows], r_out),
-        load(dirn, d_out), load(near, a_out),
+        load(vs.at[:, own_rows], d_out), load(near, a_out),
     ]
-    sum_step(curve, 2)
     known = times_f32(times_f32(plus_t, m1), plus) - 2.0 * sym(times_f32(times_f32(plus_t, m2), alpha))
     known = known + times_f32(times_f32(alpha_t, m2), alpha)
     bends = unfolded(sum_step(curve, 3))
@@ -698,12 +699,34 @@
             copy.wait_send()
 
 
-def finish(coef, x0, r1, direction, image, x_out, r_out):
-    last_s = stack(coef[:, :CLS])
-    high, low = split(direction[...])
-    x_out[...] = x0[...] + times(last_s, high, low)
-    high, low = split(image[...])
-    r_out[...] = r1[...] - times(last_s, high, low)
+def finish(coef, x0, r1, direction, image, x_out, r_out, cv, xv, rv, dv, av, in_sem, out_sem):
+    count = LV // 2
+    refs = ((direction, dv), (image, av), (x0, xv), (r1, rv))
+    chunks = [pl.ds(j * 2 * LEAF, 2 * LEAF) for j in range(count)]
+    loads = [pltpu.make_async_copy(coef, cv, in_sem.at[4 * count])]
+    for j in range(count):
+        for i, (src, dst) in enumerate(refs):
+            loads.append(
+                pltpu.make_async_copy(src.at[:, chunks[j]], dst.at[:, chunks[j]], in_sem.at[4 * j + i])
+            )
+    for copy in loads:
+        copy.start()
+    loads[0].wait()
+    last_s = stack(cv[:, :CLS])
+    stores = []
+    for j in range(count):
+        for copy in loads[4 * j + 1 : 4 * j + 5]:
+            copy.wait()
+        part = chunks[j]
+        xv[:, part] = xv[:, part] + times(last_s, dv[:CLS, part], dv[CLS:, part])
+        high, low = split(av[:, part])
+        rv[:, part] = rv[:, part] - times(last_s, high, low)
+        for i, (src, dst) in enumerate(((xv, x_out), (rv, r_out))):
+            copy = pltpu.make_async_copy(src.at[:, part], dst.at[:, part], out_sem.at[2 * j + i])
+            copy.start()
+            stores.append(copy)
+    for copy in stores:
+        copy.wait()
 
 
 def solution(mesh):
@@ -712,9 +735,10 @@
 
     def device(points, right_side, neighbours, leaf_interp, leaf_skeleton, node_skeleton, node_gain, transfer):
         out = jax.ShapeDtypeStruct(right_side.shape, F32)
+        both = jax.ShapeDtypeStruct((2 * CLS, LV * LEAF), BF16)
         x0, r1, direction, image, coef = pl.pallas_call(
             body,
-            out_shape=(out, out, out, out, jax.ShapeDtypeStruct((CLS, 128), F32)),
+            out_shape=(out, out, both, out, jax.ShapeDtypeStruct((CLS, 128), F32)),
             in_specs=[
                 any_space, any_space, pl.BlockSpec(memory_space=pltpu.SMEM), any_space,
                 any_space, any_space, any_space, any_space,
@@ -729,7 +753,6 @@
                 vmem((28, LEAF, LEAF), BF16),
                 vmem((CLS, WIDE), F32),
                 vmem((CLS, WIDE), F32),
-                vmem((CLS, LV * LEAF), F32),
                 vmem((CLS, LV * LEAF), F32),
                 vmem((2 * CLS, WIDE), BF16),
                 vmem((LV, LEAF, SKEL), F32),
@@ -757,13 +780,15 @@
                 collective_id=0, has_side_effects=True, vmem_limit_bytes=67043328
             ),
         )(points, right_side, neighbours, leaf_interp, leaf_skeleton, node_skeleton, node_gain, transfer)
-        block = pl.BlockSpec((CLS, 2 * LEAF), lambda j: (0, j))
         return pl.pallas_call(
             finish,
-            grid=(LV // 2,),
             out_shape=(out, out),
-            in_specs=[pl.BlockSpec((CLS, 128), lambda j: (0, 0)), block, block, block, block],
-            out_specs=(block, block),
+            in_specs=[any_space] * 5,
+            out_specs=(any_space, any_space),
+            scratch_shapes=[vmem((CLS, 128), F32)]
+            + [vmem((CLS, LV * LEAF), F32)] * 2
+            + [vmem((2 * CLS, LV * LEAF), BF16), vmem((CLS, LV * LEAF), F32)]
+            + [pltpu.SemaphoreType.DMA((2 * LV + 1,)), pltpu.SemaphoreType.DMA((LV,))],
         )(coef, x0, r1, direction, image)
 
     in_specs = (

time: 109 us -> 102 us (0.936)
  Pallas kernels: 108 us -> 101 us
    pallas_call x2, Pallas kernels: 108 us -> 101 us  [the longest x1 97.4 us: device(): pl.pallas_call(body, out_shape=(out, out, both, out, jax.ShapeDtypeStruct...]
where the time goes in v4:
time: 102 us
  Pallas kernels  101 us (99%)
    pallas_call x1, Pallas kernels, device(): pl.pallas_call(body, out_shape=(out, out, both, out, jax.ShapeDtypeStruct...  97.4 us
    pallas_call x1, Pallas kernels, device(): pl.pallas_call(finish, out_shape=(out, out), in_specs=[any_space] * 5, ou...  3.54 us

profile of v4, /device:TPU:0, one launch (start us, length us, event | category | flops | bytes accessed | tf_op | source)
XLA Modules:
  0.0 101.8 jit_solution(12715535552765223982)
XLA Ops:
  0.6 97.4 %shard_map.95 = (f32[64,4096]{1,0:T(8,128)}, f32[64,4096]{1,0:T(8,128)}, bf16[128,4096]{1,0:T(8,128)(2,1)}, f32[64,4096]{1,0:T(8,128)}, f32[64,128]{1,0:T(8,128)}) custom-call(f32[4096,128]{1,0:T(8,128)} %points.1, f32[64,4096]{1,0:T(8,128)} %right_side.1, s32[8,5]{1,0:T(8,128)} %neighbours.1, f32[8,512,256]{2,1,0:T(8,128)} %leaf_interp.1, ...), custom_call_target="tpu_custom_call" | custom-call | tf_op jit(solution)/shard_map/pallas_call | solution.py:739
  98.1 3.5 %shard_map.96 = (f32[64,4096]{1,0:T(8,128)}, f32[64,4096]{1,0:T(8,128)}) custom-call(f32[64,128]{1,0:T(8,128)} %get-tuple-element.7.coef, f32[64,4096]{1,0:T(8,128)} %get-tuple-element.8.x0, f32[64,4096]{1,0:T(8,128)} %get-tuple-element.9.r1, bf16[128,4096]{1,0:T(8,128)(2,1)} %get-tuple-element.10.direction, f32[64,4096]{1,0:T(8,128)} %get-tuple-element.11.image), custom_call_target="tpu_custom_call" | custom-call | tf_op jit(solution)/shard_map/pallas_call | solution.py:783

commit v5 on v4

--- a/solution.py
+++ b/solution.py
@@ -534,9 +534,9 @@
         return solve(m, jnp.where(row == col, 1.0, 0.0).astype(F32))[:, CLS:]
 
     loop2(2, 10, prepare)
+    own4, tiles3, copy_s = skel_core()
     far_tiles([(i, *pair) for i, pair in enumerate(pairs)])
     loop(0, 2, build)
-    own4, tiles3, copy_s = skel_core()
     load_b.wait()
 
     def split_b(e):

time: 102 us -> 102 us (level)
  no operation moved by 1% of the time
where the time goes in v5:
time: 102 us
  Pallas kernels  101 us (99%)
    pallas_call x1, Pallas kernels, device(): pl.pallas_call(body, out_shape=(out, out, both, out, jax.ShapeDtypeStruct...  97.4 us
    pallas_call x1, Pallas kernels, device(): pl.pallas_call(finish, out_shape=(out, out), in_specs=[any_space] * 5, ou...  3.52 us

profile of v5, /device:TPU:0, one launch (start us, length us, event | category | flops | bytes accessed | tf_op | source)
XLA Modules:
  0.0 101.7 jit_solution(12828264465752259397)
XLA Ops:
  0.6 97.4 %shard_map.95 = (f32[64,4096]{1,0:T(8,128)}, f32[64,4096]{1,0:T(8,128)}, bf16[128,4096]{1,0:T(8,128)(2,1)}, f32[64,4096]{1,0:T(8,128)}, f32[64,128]{1,0:T(8,128)}) custom-call(f32[4096,128]{1,0:T(8,128)} %points.1, f32[64,4096]{1,0:T(8,128)} %right_side.1, s32[8,5]{1,0:T(8,128)} %neighbours.1, f32[8,512,256]{2,1,0:T(8,128)} %leaf_interp.1, ...), custom_call_target="tpu_custom_call" | custom-call | tf_op jit(solution)/shard_map/pallas_call | solution.py:739
  98.0 3.5 %shard_map.96 = (f32[64,4096]{1,0:T(8,128)}, f32[64,4096]{1,0:T(8,128)}) custom-call(f32[64,128]{1,0:T(8,128)} %get-tuple-element.7.coef, f32[64,4096]{1,0:T(8,128)} %get-tuple-element.8.x0, f32[64,4096]{1,0:T(8,128)} %get-tuple-element.9.r1, bf16[128,4096]{1,0:T(8,128)(2,1)} %get-tuple-element.10.direction, f32[64,4096]{1,0:T(8,128)} %get-tuple-element.11.image), custom_call_target="tpu_custom_call" | custom-call | tf_op jit(solution)/shard_map/pallas_call | solution.py:783
